TPU v7x, 128 devices: a whole 4x4x4 slice. The times are simulated.
128 devices in a mesh: gx: 4 (over x), gy: 8 (over y, core), gz: 4 (over z).
Axes of the slice: x: 4, y: 4, z: 4, core: 2. Of those that a mesh axis runs over, the one named last changes fastest.
Arguments:
- labels: int32 [128, 512, 512], P('gx', 'gy', 'gz'), may hold values from 0 to 7
- conductivity: float32 [7, 8], replicated, may hold values from -0.08 to 2, as said below
- right_side: float32 [128, 512, 512], P('gx', 'gy', 'gz'), may hold values from -18 to 18
Outputs:
- solution: float32 [128, 512, 512], P('gx', 'gy', 'gz')
Inputs may be any that keep to these rules, and one draw needn't show every extreme that they name: `conductivity`: rows 0 to 2 are positive, rows 3 to 5 have magnitude at most 0.08, row 6 is at least 0.5.
All inputs are finite; a program needn't handle non-finite values.
Results may differ from a plain program's by a relative error of at most 0.0001.
Values sent between devices are 32-bit elements; how exact they have to be, the bound alone decides.
A program may use at most 128 MiB of HBM per device.

v0:
```python
import functools

import jax
import jax.numpy as jnp
from jax import lax
from jax.sharding import Mesh
from jax.sharding import PartitionSpec as P

ITERS = 3
GX_GY_GZ = ("gx", "gy_0", "gy_1", "gz")
GY = ("gy_0", "gy_1")


def with_halo(cells, sides, width):
    for axis, dim in sides:
        count = lax.axis_size(axis)
        ends = count - 1
        head = lax.slice_in_dim(cells, 0, width, axis=dim)
        tail = lax.slice_in_dim(cells, cells.shape[dim] - width, cells.shape[dim], axis=dim)
        cells = jnp.concatenate(
            [
                lax.ppermute(tail, axis, [(i, (i + 1) % count) for i in range(ends)]),
                cells,
                lax.ppermute(head, axis, [((i + 1) % count, i) for i in range(ends)]),
            ],
            axis=dim,
        )
    return cells


def by_axis(shard, axes):
    return functools.reduce(lax.psum, axes, shard)


def neighbour_value(arr, shift_x, shift_y, shift_z, cell_grid):
    size_x, size_y, size_z = cell_grid
    return arr[
        ...,
        1 + shift_x : 1 + shift_x + size_x,
        1 + shift_y : 1 + shift_y + size_y,
        1 + shift_z : 1 + shift_z + size_z,
    ]


def stencil_apply(padded_value, padded_sigma, self_coefficient):
    cell_grid = self_coefficient.shape
    value_entry = neighbour_value(padded_value, 0, 0, 0, cell_grid)
    total_flux = self_coefficient * value_entry
    for axis in range(3):
        for sign in (-1, 1):
            stencil_offset = [0, 0, 0]
            stencil_offset[axis] = sign
            face_flux = 0.5 * (
                neighbour_value(padded_sigma[axis], 0, 0, 0, cell_grid)
                + neighbour_value(
                    padded_sigma[axis],
                    stencil_offset[0],
                    stencil_offset[1],
                    stencil_offset[2],
                    cell_grid,
                )
            )
            total_flux = total_flux + face_flux * (
                value_entry
                - neighbour_value(
                    padded_value, stencil_offset[0], stencil_offset[1], stencil_offset[2], cell_grid
                )
            )
    for first, second, comp in ((0, 1, 3), (0, 2, 4), (1, 2, 5)):
        for sign_a in (-1, 1):
            for sign_b in (-1, 1):
                stencil_offset = [0, 0, 0]
                stencil_offset[first] = sign_a
                stencil_offset[second] = sign_b
                cross_term = (
                    0.25
                    * sign_a
                    * sign_b
                    * (
                        neighbour_value(padded_sigma[comp], 0, 0, 0, cell_grid)
                        + neighbour_value(
                            padded_sigma[comp],
                            stencil_offset[0],
                            stencil_offset[1],
                            stencil_offset[2],
                            cell_grid,
                        )
                    )
                )
                total_flux = total_flux - cross_term * neighbour_value(
                    padded_value, stencil_offset[0], stencil_offset[1], stencil_offset[2], cell_grid
                )
    return total_flux


def diagonal_of(padded_sigma, self_coefficient):
    cell_grid = self_coefficient.shape
    total_flux = self_coefficient
    for axis in range(3):
        for sign in (-1, 1):
            stencil_offset = [0, 0, 0]
            stencil_offset[axis] = sign
            total_flux = total_flux + 0.5 * (
                neighbour_value(padded_sigma[axis], 0, 0, 0, cell_grid)
                + neighbour_value(
                    padded_sigma[axis],
                    stencil_offset[0],
                    stencil_offset[1],
                    stencil_offset[2],
                    cell_grid,
                )
            )
    return total_flux


def lookup(shifted, conductivity):
    total_flux = jnp.zeros((7,) + shifted.shape, jnp.float32)
    for label in range(conductivity.shape[1]):
        hit = (shifted == label + 1).astype(jnp.float32)
        total_flux = total_flux + hit[None] * conductivity[:, label][:, None, None, None]
    return total_flux


def apply_operator(field, padded_sigma, self_coefficient):
    field_pad = with_halo(field, (("gx", 0), (GY, 1), ("gz", 2)), 1)
    return stencil_apply(field_pad, padded_sigma, self_coefficient)


def local(labels, conductivity, right_side):
    shifted = labels + 1
    shifted_pad = with_halo(shifted, (("gx", 0), (GY, 1), ("gz", 2)), 1)
    table_pad = lookup(shifted_pad, conductivity)
    padded_sigma = table_pad[:6]
    self_coefficient = table_pad[6, 1:-1, 1:-1, 1:-1]
    diag = diagonal_of(padded_sigma, self_coefficient)
    solution = jnp.zeros_like(right_side)
    residual = right_side
    precond = residual / diag
    applied = apply_operator(precond, padded_sigma, self_coefficient)
    gamma_old = jnp.float32(1.0)
    alpha_old = jnp.float32(1.0)
    direction = precond
    for step in range(ITERS):
        gamma, delta = (
            by_axis(jnp.sum(residual * precond), GX_GY_GZ),
            by_axis(jnp.sum(applied * precond), GX_GY_GZ),
        )
        if step + 1 < ITERS:
            scaled = applied / diag
            product = apply_operator(scaled, padded_sigma, self_coefficient)
        if step == 0:
            alpha = gamma / delta
            direction = precond
            along_z = product
            along_q = scaled
            along_s = applied
        else:
            ratio = gamma / gamma_old
            alpha = gamma / (delta - ratio * gamma / alpha_old)
            direction = precond + ratio * direction
            if step + 1 < ITERS:
                along_z = product + ratio * along_z
                along_q = scaled + ratio * along_q
                along_s = applied + ratio * along_s
        solution = solution + alpha * direction
        if step + 1 < ITERS:
            residual = residual - alpha * along_s
            precond = precond - alpha * along_q
            applied = applied - alpha * along_z
        gamma_old = gamma
        alpha_old = alpha
    return solution


def solution(mesh):
    finer = Mesh(
        mesh.devices.reshape(mesh.shape["gx"], 4, 2, mesh.shape["gz"]), ("gx", "gy_0", "gy_1", "gz")
    )
    in_specs = (P("gx", GY, "gz"), P(), P("gx", GY, "gz"))
    out_specs = P("gx", GY, "gz")
    return jax.shard_map(local, mesh=finer, in_specs=in_specs, out_specs=out_specs, check_vma=False)
```

profile of v0, /device:TPU:0, one launch (start us, length us, event | category | flops | bytes accessed | tf_op | source)
XLA Modules:
  0.0 381.2 jit_solution(2394452676744524515)
XLA Ops:
  6.4 4.2 %collective-permute-done.1 = s32[1,64,128]{2,1,0:T(8,128)S(1)} collective-permute-done((s32[1,64,128]{2,1,0:T(8,128)S(1)}, s32[1,64,128]{2,1,0:T(8,128)S(1)}, u32[]{:S(2)}, u32[]{:S(2)}) %collective-permute-start.1) | collective-permute-done | bytes 32800 | tf_op jit(solution)/shard_map/ppermute | solution.py:24
  22.0 4.5 %collective-permute-start.4 = (s32[34,66,1]{1,0,2:T(8,128)S(1)}, s32[34,66,1]{1,0,2:T(8,128)S(1)}, u32[]{:S(2)}, u32[]{:S(2)}) collective-permute-start(s32[34,66,1]{1,0,2:T(8,128)S(1)} %copy.67), channel_id=1, source_target_pairs={{0,1},{1,2},{2,3},{4,5},{5,6},{6,7},{8,9},{9,10},{10,11},{12,13},{... | collective-permute-start | bytes 26936 | tf_op jit(solution)/shard_map/ppermute | solution.py:22
  34.3 7.6 %compare_convert_fusion.6 = (f32[34,66,130]{1,2,0:T(8,128)}, f32[34,66,130]{1,2,0:T(8,128)}, f32[34,66,130]{1,2,0:T(8,128)}, f32[34,66,130]{1,2,0:T(8,128)}, f32...) fusion(s32[34,66,130]{1,2,0:T(8,128)} %get-tuple-element.53), kind=kLoop, calls=%fused_computation.20 | loop fusion | flops 4084080 | bytes 9335040 | tf_op jit(solution)/shard_map/convert_element_type | solution.py:119
  49.4 3.7 copy.76
  56.8 3.8 copy.74
  68.0 16.9 %multiply_add_fusion = f32[7,34,66,130]{3,2,1,0:T(8,128)} fusion(f32[7]{0:T(128)S(1)} %get-tuple-element.15, f32[34,66,130]{2,1,0:T(8,128)} %copy.78, f32[7]{0:T(128)S(1)} %get-tuple-element.16, f32[34,66,130]{2,1,0:T(8,128)} %copy.77, f32[7]{0:T(128)S(1)} %get-tuple-element.10, f32[34,66,130]{2,1,0:T(8,128)} %copy.76, f32[7]{0:T(128)S(1)} %get-tuple-element.11, ...), kind=kLoop, calls=%fused_computation | loop fusion | flops 30630600 | bytes 17503424 | tf_op jit(solution)/shard_map/add | solution.py:120
  84.9 10.0 %slice_bitcast_fusion.2 = (f32[34,66,130]{2,1,0:T(8,128)S(1)}, f32[34,66,130]{2,1,0:T(8,128)}, f32[34,66,130]{2,1,0:T(8,128)}, f32[34,66,130]{2,1,0:T(8,128)}, f...) fusion(f32[7,34,66,130]{3,2,1,0:T(8,128)} %multiply_add_fusion), kind=kLoop, calls=%fused_computation.3 | loop fusion | bytes 14002560 | tf_op jit(solution)/shard_map/squeeze | solution.py:80
  94.9 12.8 %fusion.104 = (f32[32,64,128]{2,1,0:T(8,128)S(1)}, f32[32,64,128]{2,1,0:T(8,128)}, f32[32,64,128]{2,1,0:T(8,128)}, f32[32,64,128]{2,1,0:T(8,128)}, f32[32,64,128...) fusion(f32[32,64,128]{2,1,0:T(8,128)} %param.5, ...), kind=kLoop, calls=%fused_computation.239 | loop fusion | flops 4980736 | bytes 19922944 | tf_op jit(solution)/shard_map/div | solution.py:138
  112.7 4.3 %collective-permute-done.7 = f32[1,64,128]{2,1,0:T(8,128)S(1)} collective-permute-done((f32[1,64,128]{2,1,0:T(8,128)S(1)}, f32[1,64,128]{2,1,0:T(8,128)S(1)}, u32[]{:S(2)}, u32[]{:S(2)}) %collective-permute-start.7) | collective-permute-done | bytes 32800 | tf_op jit(solution)/shard_map/ppermute | solution.py:24
  120.3 5.1 %collective-permute-done.9 = f32[34,1,128]{2,1,0:T(1,128)S(1)} collective-permute-done((f32[34,1,128]{2,1,0:T(1,128)S(1)}, f32[34,1,128]{2,1,0:T(1,128)S(1)}, u32[]{:S(2)}, u32[]{:S(2)}) %collective-permute-start.9) | collective-permute-done | bytes 17440 | tf_op jit(solution)/shard_map/ppermute | solution.py:24
  134.1 5.4 %collective-permute-start.10 = (f32[34,66,1]{1,2,0:T(1,128)}, f32[34,66,1]{1,2,0:T(1,128)}, u32[]{:S(2)}, u32[]{:S(2)}) collective-permute-start(f32[34,66,1]{1,2,0:T(1,128)} %copy.79), channel_id=1, source_target_pairs={{0,1},{1,2},{2,3},{4,5},{5,6},{6,7},{8,9},{9,10},{10,11},{12,13},{... | collective-permute-start | bytes 26936 | tf_op jit(solution)/shard_map/ppermute | solution.py:22
  146.7 3.8 maximum_maximum_fusion
  150.8 10.2 %multiply_reduce_fusion.3 = (f32[]{:T(128)}, f32[]{:T(128)}, f32[32,64,128]{2,1,0:T(8,128)S(1)}) fusion(f32[32,64,128]{2,1,0:T(8,128)S(1)} %get-tuple-element.44, f32[32,64,128]{2,1,0:T(8,128)} %param.5, f32[34,66,129]{2,1,0:T(8,128)S(1)} %get-tuple-element.80, f32[34,66,130]{2,1,0:T(8,128)S(1)} %copy-done, f32[34,66,129]{2,1,0:T(8,128)S(1)} %get-tuple-element.79, ...), kind=kLoop, calls=%fused_computation.214 | loop fusion | flops 19136512 | bytes 43057160 | tf_op jit(solution)/shard_map/reduce_sum | solution.py:146
  166.0 4.2 %collective-permute-done.13 = f32[1,64,128]{2,1,0:T(8,128)S(1)} collective-permute-done((f32[1,64,128]{2,1,0:T(8,128)S(1)}, f32[1,64,128]{2,1,0:T(8,128)S(1)}, u32[]{:S(2)}, u32[]{:S(2)}) %collective-permute-start.13) | collective-permute-done | bytes 32800 | tf_op jit(solution)/shard_map/ppermute | solution.py:24
  175.4 8.6 %all-reduce.8 = (f32[]{:T(128)}, f32[]{:T(128)}) all-reduce(f32[]{:T(128)} %get-tuple-element.8, f32[]{:T(128)} %get-tuple-element.7), channel_id=1, replica_groups=mesh['gx'=4,'gy_0'=4,'gy_1'=2,'gz'=4] {'gx'}, use_global_device_ids=true, to_apply=%region_1.0 | all-reduce | flops 2 | bytes 16 | tf_op jit(solution)/shard_map/psum | solution.py:32
  184.0 13.0 %all-reduce.5 = (f32[]{:T(128)}, f32[]{:T(128)}) all-reduce(f32[]{:T(128)} %get-tuple-element.33, f32[]{:T(128)} %get-tuple-element.34), channel_id=1, replica_groups=mesh['gx'=4,'gy_0'=4,'gy_1'=2,'gz'=4] {'gy_0'}, use_global_device_ids=true, to_apply=%region_2.0 | all-reduce | flops 2 | bytes 16 | tf_op jit(solution)/shard_map/psum | solution.py:32
  200.1 12.4 %all-reduce.2 = (f32[]{:T(128)}, f32[]{:T(128)}) all-reduce(f32[]{:T(128)} %get-tuple-element.39, f32[]{:T(128)} %get-tuple-element.40), channel_id=1, replica_groups=mesh['gx'=4,'gy_0'=4,'gy_1'=2,'gz'=4] {'gz'}, use_global_device_ids=true, to_apply=%region_4.0 | all-reduce | flops 2 | bytes 16 | tf_op jit(solution)/shard_map/psum | solution.py:32
  223.2 5.2 %collective-permute-start.16 = (f32[34,66,1]{1,2,0:T(1,128)}, f32[34,66,1]{1,2,0:T(1,128)}, u32[]{:S(2)}, u32[]{:S(2)}) collective-permute-start(f32[34,66,1]{1,2,0:T(1,128)} %copy.83), channel_id=1, source_target_pairs={{0,1},{1,2},{2,3},{4,5},{5,6},{6,7},{8,9},{9,10},{10,11},{12,13},{... | collective-permute-start | bytes 26936 | tf_op jit(solution)/shard_map/ppermute | solution.py:22
  236.1 4.1 %maximum_maximum_fusion.1 = (f32[34,66,129]{2,1,0:T(8,128)S(1)}, f32[34,66,129]{2,1,0:T(8,128)S(1)}) fusion(f32[34,1,128]{2,1,0:T(1,128)} %collective-permute-done.15, f32[1,64,128]{2,1,0:T(8,128)} %copy-done.26, f32[32,64,128]{2,1,0:T(8,128)} %copy-done.6, f32[1,64,128]{2,1,0:T(8,128)} %copy-done.24, f32[34,1,128]{2,1,0:T(1,128)} %collective-permute-done.14, ...), kind=kLoop, calls=%fused_computation.9 | loop fusion | flops 2894760 | bytes 3482688 | tf_op jit(solution)/shard_map/concatenate | solution.py:20
  240.9 9.7 %fusion.101 = (f32[32,64,128]{2,1,0:T(8,128)S(1)}, f32[32,64,128]{2,1,0:T(8,128)S(1)}) fusion(f32[32,64,128]{2,1,0:T(8,128)S(1)} %copy-done.16, f32[32,64,128]{2,1,0:T(8,128)S(1)} %copy-done.10, f32[]{:T(128)S(6)} %div.31, f32[34,66,129]{2,1,0:T(8,128)S(1)} %get-tuple-element.78, f32[34,66,130]{2,1,0:T(8,128)S(1)} %copy-done.1, ...), kind=kLoop, calls=%fused_computation.218 | loop fusion | flops 18874368 | bytes 45154308 | tf_op jit(solution)/shard_map/div | solution.py:149
  251.4 4.5 %collective-permute-start.18 = (f32[1,64,128]{2,1,0:T(8,128)}, f32[1,64,128]{2,1,0:T(8,128)}, u32[]{:S(2)}, u32[]{:S(2)}) collective-permute-start(f32[1,64,128]{2,1,0:T(8,128)} %get-tuple-element.95), channel_id=1, source_target_pairs={{0,32},{32,64},{64,96},{1,33},{33,65},{65,97},{2,34},{34,66},{66,9... | collective-permute-start | bytes 98312 | tf_op jit(solution)/shard_map/ppermute | solution.py:22
  258.4 10.9 %all-reduce.7 = (f32[]{:T(128)}, f32[]{:T(128)}) all-reduce(f32[]{:T(128)} %get-tuple-element.6, f32[]{:T(128)} %get-tuple-element.5), channel_id=1, replica_groups=mesh['gx'=4,'gy_0'=4,'gy_1'=2,'gz'=4] {'gx'}, use_global_device_ids=true, to_apply=%region_11.0 | all-reduce | flops 2 | bytes 16 | tf_op jit(solution)/shard_map/psum | solution.py:32
  269.3 8.4 %all-reduce.4 = (f32[]{:T(128)}, f32[]{:T(128)}) all-reduce(f32[]{:T(128)} %get-tuple-element.31, f32[]{:T(128)} %get-tuple-element.32), channel_id=1, replica_groups=mesh['gx'=4,'gy_0'=4,'gy_1'=2,'gz'=4] {'gy_0'}, use_global_device_ids=true, to_apply=%region_12.0 | all-reduce | flops 2 | bytes 16 | tf_op jit(solution)/shard_map/psum | solution.py:32
  280.9 8.6 %all-reduce.1 = (f32[]{:T(128)}, f32[]{:T(128)}) all-reduce(f32[]{:T(128)} %get-tuple-element.37, f32[]{:T(128)} %get-tuple-element.38), channel_id=1, replica_groups=mesh['gx'=4,'gy_0'=4,'gy_1'=2,'gz'=4] {'gz'}, use_global_device_ids=true, to_apply=%region_14.0 | all-reduce | flops 2 | bytes 16 | tf_op jit(solution)/shard_map/psum | solution.py:32
  297.9 3.8 %multiply_reduce_fusion = f32[]{:T(128)} fusion(f32[32,64,128]{2,1,0:T(8,128)} %copy-done.9, f32[32,64,128]{2,1,0:T(8,128)} %param.5, f32[]{:T(128)S(6)} %div.33, f32[]{:T(128)S(6)} %div.35, f32[]{:T(128)S(6)} %div.31, f32[32,64,128]{2,1,0:T(8,128)} %copy-done.17, f32[32,64,128]{2,1,0:T(8,128)} %copy-done.6, f32[32,64,128]{2,1,0:T(8,128)} %get-tuple-element.45, ...), kind=kLoop, calls=%fused_computation.207 | loop fusion | flops 4456447 | bytes 6291472 | tf_op jit(solution)/shard_map/reduce_sum | solution.py:145
  310.4 5.1 %collective-permute-start.22 = (f32[34,66,1]{1,2,0:T(1,128)}, f32[34,66,1]{1,2,0:T(1,128)}, u32[]{:S(2)}, u32[]{:S(2)}) collective-permute-start(f32[34,66,1]{1,2,0:T(1,128)} %copy.87), channel_id=1, source_target_pairs={{0,1},{1,2},{2,3},{4,5},{5,6},{6,7},{8,9},{9,10},{10,11},{12,13},{... | collective-permute-start | bytes 26936 | tf_op jit(solution)/shard_map/ppermute | solution.py:22
  323.4 4.1 %maximum_maximum_fusion.2 = (f32[34,66,129]{2,1,0:T(8,128)S(1)}, f32[34,66,129]{2,1,0:T(8,128)S(1)}) fusion(f32[34,1,128]{2,1,0:T(1,128)} %copy-done.35, f32[1,64,128]{2,1,0:T(8,128)} %collective-permute-done.19, f32[32,64,128]{2,1,0:T(8,128)} %copy-done.12, f32[1,64,128]{2,1,0:T(8,128)} %collective-permute-done.18, f32[34,1,128]{2,1,0:T(1,128)} %copy-done.33, ...), kind=kLoop, calls=%fused_computation.11 | loop fusion | flops 2894760 | bytes 3482688 | tf_op jit(solution)/shard_map/concatenate | solution.py:20
  328.3 10.9 %fusion.5 = f32[]{:T(128)} fusion(f32[34,66,129]{2,1,0:T(8,128)S(1)} %get-tuple-element.76, f32[34,66,129]{2,1,0:T(8,128)S(1)} %get-tuple-element.75, f32[34,65,128]{2,1,0:T(8,128)} %get-tuple-element.82, f32[34,65,128]{2,1,0:T(8,128)} %get-tuple-element.81, f32[32,64,128]{2,1,0:T(8,128)} %get-tuple-element.51, f32[32,64,128]{2,1,0:T(8,128)S(1)} %copy-done.14, ...), kind=kLoop, calls=%fused_computation.38 | loop fusion | flops 22020096 | bytes 46202896 | tf_op jit(solution)/shard_map/reduce_sum | solution.py:146
  339.1 8.4 %all-reduce.6 = (f32[]{:T(128)}, f32[]{:T(128)}) all-reduce(f32[]{:T(128)} %multiply_reduce_fusion, f32[]{:T(128)} %fusion.5), channel_id=1, replica_groups=mesh['gx'=4,'gy_0'=4,'gy_1'=2,'gz'=4] {'gx'}, use_global_device_ids=true, to_apply=%region_21.0 | all-reduce | flops 2 | bytes 16 | tf_op jit(solution)/shard_map/psum | solution.py:32
  347.6 13.3 %all-reduce.3 = (f32[]{:T(128)}, f32[]{:T(128)}) all-reduce(f32[]{:T(128)} %get-tuple-element.29, f32[]{:T(128)} %get-tuple-element.30), channel_id=1, replica_groups=mesh['gx'=4,'gy_0'=4,'gy_1'=2,'gz'=4] {'gy_0'}, use_global_device_ids=true, to_apply=%region_22.0 | all-reduce | flops 2 | bytes 16 | tf_op jit(solution)/shard_map/psum | solution.py:32
  364.0 9.6 %all-reduce = (f32[]{:T(128)}, f32[]{:T(128)}) all-reduce(f32[]{:T(128)} %get-tuple-element.35, f32[]{:T(128)} %get-tuple-element.36), channel_id=1, replica_groups=mesh['gx'=4,'gy_0'=4,'gy_1'=2,'gz'=4] {'gz'}, use_global_device_ids=true, to_apply=%region_24.0 | all-reduce | flops 2 | bytes 16 | tf_op jit(solution)/shard_map/psum | solution.py:32
  377.3 3.8 multiply_add_fusion.1
  (167 shorter events, 130.1 us)
Async XLA Ops:
  1.3 5.1 %collective-permute-start = (s32[1,64,128]{2,1,0:T(8,128)S(1)}, s32[1,64,128]{2,1,0:T(8,128)S(1)}, u32[]{:S(2)}, u32[]{:S(2)}) collective-permute-start(s32[1,64,128]{2,1,0:T(8,128)S(1)} %get-tuple-element.101), channel_id=1, source_target_pairs={{0,32},{32,64},{64,96},{1,33},{33,65},{65,97},{2,34},{34,66},{66,9... | collective-permute-start | bytes 98312 | tf_op jit(solution)/shard_map/ppermute | solution.py:22
  4.8 5.8 %collective-permute-start.1 = (s32[1,64,128]{2,1,0:T(8,128)S(1)}, s32[1,64,128]{2,1,0:T(8,128)S(1)}, u32[]{:S(2)}, u32[]{:S(2)}) collective-permute-start(s32[1,64,128]{2,1,0:T(8,128)S(1)} %get-tuple-element.102), channel_id=1, source_target_pairs={{32,0},{64,32},{96,64},{33,1},{65,33},{97,65},{34,2},{66,34},{98,6... | collective-permute-start | bytes 98312 | tf_op jit(solution)/shard_map/ppermute | solution.py:24
  10.8 3.5 collective-permute-start.2
  12.1 4.9 %collective-permute-start.3 = (s32[34,1,128]{2,0,1:T(8,128)S(1)}, s32[34,1,128]{2,0,1:T(8,128)S(1)}, u32[]{:S(2)}, u32[]{:S(2)}) collective-permute-start(s32[34,1,128]{2,0,1:T(8,128)S(1)} %copy.92), channel_id=1, source_target_pairs={{4,0},{8,4},{12,8},{16,12},{20,16},{24,20},{28,24},{5,1},{9,5},{13... | collective-permute-start | bytes 52232 | tf_op jit(solution)/shard_map/ppermute | solution.py:24
  19.1 9.0 %copy-start.18 = (s32[34,1,128]{1,2,0:T(8,128)S(1)}, s32[34,1,128]{1,2,0:T(8,128)}, u32[]{:S(2)}) copy-start(s32[34,1,128]{1,2,0:T(8,128)} %copy.64) | copy-start | bytes 52228
  19.1 9.0 %copy-start.19 = (s32[34,1,128]{1,2,0:T(8,128)S(1)}, s32[34,1,128]{1,2,0:T(8,128)}, u32[]{:S(2)}) copy-start(s32[34,1,128]{1,2,0:T(8,128)} %copy.66) | copy-start | bytes 52228
  20.6 6.3 %collective-permute-start.5 = (s32[34,66,1]{1,0,2:T(8,128)S(1)}, s32[34,66,1]{1,0,2:T(8,128)S(1)}, u32[]{:S(2)}, u32[]{:S(2)}) collective-permute-start(s32[34,66,1]{1,0,2:T(8,128)S(1)} %copy.68), channel_id=1, source_target_pairs={{1,0},{2,1},{3,2},{5,4},{6,5},{7,6},{9,8},{10,9},{11,10},{13,12},{... | collective-permute-start | bytes 26936 | tf_op jit(solution)/shard_map/ppermute | solution.py:24
  22.0 6.0 %collective-permute-start.4 = (s32[34,66,1]{1,0,2:T(8,128)S(1)}, s32[34,66,1]{1,0,2:T(8,128)S(1)}, u32[]{:S(2)}, u32[]{:S(2)}) collective-permute-start(s32[34,66,1]{1,0,2:T(8,128)S(1)} %copy.67), channel_id=1, source_target_pairs={{0,1},{1,2},{2,3},{4,5},{5,6},{6,7},{8,9},{9,10},{10,11},{12,13},{... | collective-permute-start | bytes 26936 | tf_op jit(solution)/shard_map/ppermute | solution.py:22
  107.7 5.0 %collective-permute-start.6 = (f32[1,64,128]{2,1,0:T(8,128)S(1)}, f32[1,64,128]{2,1,0:T(8,128)S(1)}, u32[]{:S(2)}, u32[]{:S(2)}) collective-permute-start(f32[1,64,128]{2,1,0:T(8,128)S(1)} %get-tuple-element.99), channel_id=1, source_target_pairs={{0,32},{32,64},{64,96},{1,33},{33,65},{65,97},{2,34},{34,66},{66,9... | collective-permute-start | bytes 98312 | tf_op jit(solution)/shard_map/ppermute | solution.py:22
  111.1 5.8 %collective-permute-start.7 = (f32[1,64,128]{2,1,0:T(8,128)S(1)}, f32[1,64,128]{2,1,0:T(8,128)S(1)}, u32[]{:S(2)}, u32[]{:S(2)}) collective-permute-start(f32[1,64,128]{2,1,0:T(8,128)S(1)} %get-tuple-element.100), channel_id=1, source_target_pairs={{32,0},{64,32},{96,64},{33,1},{65,33},{97,65},{34,2},{66,34},{98,6... | collective-permute-start | bytes 98312 | tf_op jit(solution)/shard_map/ppermute | solution.py:24
  112.7 12.8 %copy-start.28 = (f32[1,64,128]{2,1,0:T(8,128)}, f32[1,64,128]{2,1,0:T(8,128)S(1)}, u32[]{:S(2)}) copy-start(f32[1,64,128]{2,1,0:T(8,128)S(1)} %collective-permute-done.6) | copy-start | bytes 98308
  116.9 8.5 %copy-start.30 = (f32[1,64,128]{2,1,0:T(8,128)}, f32[1,64,128]{2,1,0:T(8,128)S(1)}, u32[]{:S(2)}) copy-start(f32[1,64,128]{2,1,0:T(8,128)S(1)} %collective-permute-done.7) | copy-start | bytes 98308
  116.9 3.4 collective-permute-start.8
  119.0 6.4 %collective-permute-start.9 = (f32[34,1,128]{2,1,0:T(1,128)S(1)}, f32[34,1,128]{2,1,0:T(1,128)S(1)}, u32[]{:S(2)}, u32[]{:S(2)}) collective-permute-start(f32[34,1,128]{2,1,0:T(1,128)S(1)} %get-tuple-element.92), channel_id=1, source_target_pairs={{4,0},{8,4},{12,8},{16,12},{20,16},{24,20},{28,24},{5,1},{9,5},{13... | collective-permute-start | bytes 52232 | tf_op jit(solution)/shard_map/ppermute | solution.py:24
  132.8 11.6 %collective-permute-start.11 = (f32[34,66,1]{1,2,0:T(1,128)}, f32[34,66,1]{1,2,0:T(1,128)}, u32[]{:S(2)}, u32[]{:S(2)}) collective-permute-start(f32[34,66,1]{1,2,0:T(1,128)} %copy.81), channel_id=1, source_target_pairs={{1,0},{2,1},{3,2},{5,4},{6,5},{7,6},{9,8},{10,9},{11,10},{13,12},{... | collective-permute-start | bytes 26936 | tf_op jit(solution)/shard_map/ppermute | solution.py:24
  134.1 8.0 %collective-permute-start.10 = (f32[34,66,1]{1,2,0:T(1,128)}, f32[34,66,1]{1,2,0:T(1,128)}, u32[]{:S(2)}, u32[]{:S(2)}) collective-permute-start(f32[34,66,1]{1,2,0:T(1,128)} %copy.79), channel_id=1, source_target_pairs={{0,1},{1,2},{2,3},{4,5},{5,6},{6,7},{8,9},{9,10},{10,11},{12,13},{... | collective-permute-start | bytes 26936 | tf_op jit(solution)/shard_map/ppermute | solution.py:22
  150.8 10.2 %copy-start.15 = (f32[32,64,128]{2,1,0:T(8,128)S(1)}, f32[32,64,128]{2,1,0:T(8,128)}, u32[]{:S(2)}) copy-start(f32[32,64,128]{2,1,0:T(8,128)} %get-tuple-element.45) | copy-start | bytes 3145732
  161.0 9.9 %copy-start.9 = (f32[32,64,128]{2,1,0:T(8,128)}, f32[32,64,128]{2,1,0:T(8,128)S(1)}, u32[]{:S(2)}) copy-start(f32[32,64,128]{2,1,0:T(8,128)S(1)} %get-tuple-element.43) | copy-start | bytes 3145732
  161.2 8.9 %copy-start.6 = (f32[32,64,128]{2,1,0:T(8,128)}, f32[32,64,128]{2,1,0:T(8,128)S(1)}, u32[]{:S(2)}) copy-start(f32[32,64,128]{2,1,0:T(8,128)S(1)} %div.32) | copy-start | bytes 3145732
  161.3 4.7 %collective-permute-start.12 = (f32[1,64,128]{2,1,0:T(8,128)S(1)}, f32[1,64,128]{2,1,0:T(8,128)S(1)}, u32[]{:S(2)}, u32[]{:S(2)}) collective-permute-start(f32[1,64,128]{2,1,0:T(8,128)S(1)} %get-tuple-element.97), channel_id=1, source_target_pairs={{0,32},{32,64},{64,96},{1,33},{33,65},{65,97},{2,34},{34,66},{66,9... | collective-permute-start | bytes 98312 | tf_op jit(solution)/shard_map/ppermute | solution.py:22
  164.4 5.8 %collective-permute-start.13 = (f32[1,64,128]{2,1,0:T(8,128)S(1)}, f32[1,64,128]{2,1,0:T(8,128)S(1)}, u32[]{:S(2)}, u32[]{:S(2)}) collective-permute-start(f32[1,64,128]{2,1,0:T(8,128)S(1)} %get-tuple-element.98), channel_id=1, source_target_pairs={{32,0},{64,32},{96,64},{33,1},{65,33},{97,65},{34,2},{66,34},{98,6... | collective-permute-start | bytes 98312 | tf_op jit(solution)/shard_map/ppermute | solution.py:24
  170.8 43.1 %collective-permute-start.14 = (f32[34,1,128]{2,1,0:T(1,128)}, f32[34,1,128]{2,1,0:T(1,128)}, u32[]{:S(2)}, u32[]{:S(2)}) collective-permute-start(f32[34,1,128]{2,1,0:T(1,128)} %get-tuple-element.87), channel_id=1, source_target_pairs={{0,4},{4,8},{8,12},{12,16},{16,20},{20,24},{24,28},{1,5},{5,9},{9,... | collective-permute-start | bytes 52232 | tf_op jit(solution)/shard_map/ppermute | solution.py:22
  174.1 39.8 %collective-permute-start.15 = (f32[34,1,128]{2,1,0:T(1,128)}, f32[34,1,128]{2,1,0:T(1,128)}, u32[]{:S(2)}, u32[]{:S(2)}) collective-permute-start(f32[34,1,128]{2,1,0:T(1,128)} %get-tuple-element.88), channel_id=1, source_target_pairs={{4,0},{8,4},{12,8},{16,12},{20,16},{24,20},{28,24},{5,1},{9,5},{13... | collective-permute-start | bytes 52232 | tf_op jit(solution)/shard_map/ppermute | solution.py:24
  221.9 12.0 %collective-permute-start.17 = (f32[34,66,1]{1,2,0:T(1,128)}, f32[34,66,1]{1,2,0:T(1,128)}, u32[]{:S(2)}, u32[]{:S(2)}) collective-permute-start(f32[34,66,1]{1,2,0:T(1,128)} %copy.85), channel_id=1, source_target_pairs={{1,0},{2,1},{3,2},{5,4},{6,5},{7,6},{9,8},{10,9},{11,10},{13,12},{... | collective-permute-start | bytes 26936 | tf_op jit(solution)/shard_map/ppermute | solution.py:24
  223.2 8.4 %collective-permute-start.16 = (f32[34,66,1]{1,2,0:T(1,128)}, f32[34,66,1]{1,2,0:T(1,128)}, u32[]{:S(2)}, u32[]{:S(2)}) collective-permute-start(f32[34,66,1]{1,2,0:T(1,128)} %copy.83), channel_id=1, source_target_pairs={{0,1},{1,2},{2,3},{4,5},{5,6},{6,7},{8,9},{9,10},{10,11},{12,13},{... | collective-permute-start | bytes 26936 | tf_op jit(solution)/shard_map/ppermute | solution.py:22
  240.9 16.2 %copy-start.23 = (f32[32,64,128]{2,1,0:T(8,128)S(1)}, f32[32,64,128]{2,1,0:T(8,128)}, u32[]{:S(2)}) copy-start(f32[32,64,128]{2,1,0:T(8,128)} %param.5) | copy-start | bytes 3145732
  251.4 42.5 %collective-permute-start.18 = (f32[1,64,128]{2,1,0:T(8,128)}, f32[1,64,128]{2,1,0:T(8,128)}, u32[]{:S(2)}, u32[]{:S(2)}) collective-permute-start(f32[1,64,128]{2,1,0:T(8,128)} %get-tuple-element.95), channel_id=1, source_target_pairs={{0,32},{32,64},{64,96},{1,33},{33,65},{65,97},{2,34},{34,66},{66,9... | collective-permute-start | bytes 98312 | tf_op jit(solution)/shard_map/ppermute | solution.py:22
  255.9 38.0 %collective-permute-start.19 = (f32[1,64,128]{2,1,0:T(8,128)}, f32[1,64,128]{2,1,0:T(8,128)}, u32[]{:S(2)}, u32[]{:S(2)}) collective-permute-start(f32[1,64,128]{2,1,0:T(8,128)} %get-tuple-element.96), channel_id=1, source_target_pairs={{32,0},{64,32},{96,64},{33,1},{65,33},{97,65},{34,2},{66,34},{98,6... | collective-permute-start | bytes 98312 | tf_op jit(solution)/shard_map/ppermute | solution.py:24
  294.9 6.8 %collective-permute-start.20 = (f32[34,1,128]{2,1,0:T(1,128)S(1)}, f32[34,1,128]{2,1,0:T(1,128)S(1)}, u32[]{:S(2)}, u32[]{:S(2)}) collective-permute-start(f32[34,1,128]{2,1,0:T(1,128)S(1)} %get-tuple-element.83), channel_id=1, source_target_pairs={{0,4},{4,8},{8,12},{12,16},{16,20},{20,24},{24,28},{1,5},{5,9},{9,... | collective-permute-start | bytes 52232 | tf_op jit(solution)/shard_map/ppermute | solution.py:22
  296.2 5.5 %collective-permute-start.21 = (f32[34,1,128]{2,1,0:T(1,128)S(1)}, f32[34,1,128]{2,1,0:T(1,128)S(1)}, u32[]{:S(2)}, u32[]{:S(2)}) collective-permute-start(f32[34,1,128]{2,1,0:T(1,128)S(1)} %get-tuple-element.84), channel_id=1, source_target_pairs={{4,0},{8,4},{12,8},{16,12},{20,16},{24,20},{28,24},{5,1},{9,5},{13... | collective-permute-start | bytes 52232 | tf_op jit(solution)/shard_map/ppermute | solution.py:24
  309.1 12.0 %collective-permute-start.23 = (f32[34,66,1]{1,2,0:T(1,128)}, f32[34,66,1]{1,2,0:T(1,128)}, u32[]{:S(2)}, u32[]{:S(2)}) collective-permute-start(f32[34,66,1]{1,2,0:T(1,128)} %copy.89), channel_id=1, source_target_pairs={{1,0},{2,1},{3,2},{5,4},{6,5},{7,6},{9,8},{10,9},{11,10},{13,12},{... | collective-permute-start | bytes 26936 | tf_op jit(solution)/shard_map/ppermute | solution.py:24
  310.4 8.5 %collective-permute-start.22 = (f32[34,66,1]{1,2,0:T(1,128)}, f32[34,66,1]{1,2,0:T(1,128)}, u32[]{:S(2)}, u32[]{:S(2)}) collective-permute-start(f32[34,66,1]{1,2,0:T(1,128)} %copy.87), channel_id=1, source_target_pairs={{0,1},{1,2},{2,3},{4,5},{5,6},{6,7},{8,9},{9,10},{10,11},{12,13},{... | collective-permute-start | bytes 26936 | tf_op jit(solution)/shard_map/ppermute | solution.py:22
  (29 other events, 129.5 us)
where the time goes:
time: 384 us; the launch traced here: 381 us
  other arithmetic  109 us (28%)
  blocking collectives  103 us (27%)
  local copies, waits for them, and re-layouts  80.6 us (21%)
  starting transfers between devices  58.6 us (15%)
  waiting for transfers between devices  20.5 us (5%)
  between operations  10.1 us (3%)
    psum x12, blocking collectives, by_axis(): return functools.reduce(lax.psum, axes, shard)  103 us
    ppermute x12, starting transfers between devices, with_halo(): lax.ppermute(tail, axis, [(i, (i + 1) % count) for i in range(ends)])  42.7 us
    convert_element_type x8, local copies, waits for them, and re-layouts, lookup(): hit = (shifted == label + 1).astype(jnp.float32)  28.8 us
    concatenate x10, other arithmetic, with_halo(): jnp.concatenate([lax.ppermute(tail, axis, [(i, (i + 1) % count) for i in...  23.5 us
    reduce_sum x3, other arithmetic, local(): jnp.sum(applied * precond)  22.3 us
    ppermute x12, waiting for transfers between devices, with_halo(): lax.ppermute(head, axis, [((i + 1) % count, i) for i in range(ends)])  18.5 us
    add x1, other arithmetic, lookup(): total_flux + hit[None] * conductivity[:, label][:, None, None, None]  16.9 us
    ppermute x12, starting transfers between devices, with_halo(): lax.ppermute(head, axis, [((i + 1) % count, i) for i in range(ends)])  15.9 us
  transfers between devices with their start and end apart: 24, of which 9 were waited for; matrix products, arithmetic and copies ran while one was open for 6% of the time, Pallas kernels for 0%

commit v1 on v0

v1 whole, which is shorter than its diff:
```python
import functools

import jax
import jax.numpy as jnp
from jax import lax
from jax.experimental import pallas as pl
from jax.experimental.pallas import tpu as pltpu
from jax.sharding import PartitionSpec as P

MESH = pl.DeviceIdType.MESH
W = 4
LAYERS = 12
OUTSIDE = 8
DIRS = tuple((a, b) for a in (-1, 0, 1) for b in (-1, 0, 1) if (a, b) != (0, 0))
UNROLL = 2


def row_groups(lo, hi):
    starts = list(range(lo, hi - 7, 8))
    if starts[-1] + 8 < hi:
        starts.append(hi - 8)
    return starts


def group_spans(lo, hi, first, last):
    spans, done = [], first
    for start in row_groups(lo, hi):
        low, high = max(done, start), min(last, start + 8)
        done = max(done, high)
        spans.append((start, low - start, max(high, low) - start))
    return spans


def kernel(sizes, cond, lab_hbm, b_hbm, out, *scr):
    (gxn, gyn, gzn, X, Y) = sizes
    PX, PY = X + 2 * W, Y + 2 * W
    (e_lab, e_b, e_sig, e_inv, e_v, e_tmp, k_lab, k_b, k_sig, k_inv, k_v, k_tmp, kint, kt, ar, arslot,
     load_sem, s1, r1, s2, r2, sa, ra) = scr
    gx, gy, gz = lax.axis_index("gx"), lax.axis_index("gy"), lax.axis_index("gz")

    load_lab = pltpu.make_async_copy(lab_hbm, e_lab.at[pl.ds(W, X), pl.ds(W, Y), :], load_sem.at[0])
    load_b = pltpu.make_async_copy(b_hbm, e_b.at[pl.ds(W, X), pl.ds(W, Y), :], load_sem.at[1])
    load_lab.start()
    load_b.start()

    def exists(dx, dy):
        ok = None
        for pos, d, n in ((gx, dx, gxn), (gy, dy, gyn)):
            if d:
                here = (pos + d >= 0) & (pos + d < n)
                ok = here if ok is None else ok & here
        return ok

    barrier = pltpu.get_barrier_semaphore()
    for axis, pos, n in (("gy", gy, gyn), ("gx", gx, gxn), ("gz", gz, gzn)):
        for d in range(1, n):
            pl.semaphore_signal(barrier, inc=1, device_id={axis: lax.rem(pos + d, n)}, device_id_type=MESH)
    peers = gyn - 1 + gxn - 1 + gzn - 1
    for dx, dy in DIRS:
        if dx and dy:
            ok = exists(dx, dy)

            @pl.when(ok)
            def _():
                pl.semaphore_signal(barrier, inc=1, device_id={"gx": gx + dx, "gy": gy + dy}, device_id_type=MESH)

            peers = peers + ok.astype(jnp.int32)
    pl.semaphore_wait(barrier, peers)

    def region(d, n, width, arriving):
        if d == 0:
            return pl.ds(W, n)
        if arriving:
            return pl.ds(W + n, width) if d < 0 else pl.ds(W - width, width)
        return pl.ds(W, width) if d < 0 else pl.ds(W + n - width, width)

    def phase1(i, field):
        dx, dy = DIRS[i]
        ref, width = ((e_lab, W), (e_b, W - 1))[field]
        src = ref.at[region(dx, X, width, False), region(dy, Y, width, False), :]
        dst = ref.at[region(dx, X, width, True), region(dy, Y, width, True), :]
        target = {}
        if dx:
            target["gx"] = jnp.clip(gx + dx, 0, gxn - 1)
        if dy:
            target["gy"] = jnp.clip(gy + dy, 0, gyn - 1)
        return pltpu.make_async_remote_copy(
            src_ref=src, dst_ref=dst, send_sem=s1.at[i, field], recv_sem=r1.at[i, field],
            device_id=target, device_id_type=MESH)

    for field, load in ((0, load_lab), (1, load_b)):
        load.wait()
        for i, (dx, dy) in enumerate(DIRS):
            @pl.when(exists(dx, dy))
            def _():
                phase1(i, field).start()

    def fill_e(xs, nx, ys, ny):
        def body(m, c):
            e_lab[xs + m, pl.ds(ys, ny), :] = jnp.full((ny, 128), OUTSIDE, jnp.int32)
            e_b[xs + m, pl.ds(ys, ny), :] = jnp.zeros((ny, 128), jnp.float32)
            return c
        lax.fori_loop(0, nx, body, 0)

    @pl.when(gx == 0)
    def _():
        fill_e(0, W, 0, PY)

    @pl.when(gx == gxn - 1)
    def _():
        fill_e(W + X, W, 0, PY)

    @pl.when(gy == 0)
    def _():
        fill_e(0, PX, 0, W)

    @pl.when(gy == gyn - 1)
    def _():
        fill_e(0, PX, W + Y, W)

    def fill_k(side, layer):
        rows = pl.ds((side * LAYERS + layer) * PX, W * PX)
        k_lab[rows, :] = jnp.full((W * PX, 128), OUTSIDE, jnp.int32)
        k_b[rows, :] = jnp.zeros((W * PX, 128), jnp.float32)

    @pl.when(gz == 0)
    def _():
        fill_k(0, 0)

    @pl.when(gz == gzn - 1)
    def _():
        fill_k(1, 2 * W)

    for field in (0, 1):
        for i, (dx, dy) in enumerate(DIRS):
            @pl.when(exists(-dx, -dy))
            def _():
                phase1(i, field).wait_recv()

    def extract(m, c):
        for src, dst in ((e_lab, k_lab), (e_b, k_b)):
            plane = jnp.concatenate([src[m], jnp.zeros((128 - PY, 128), src.dtype)], axis=0)
            turned = plane.T
            dst[pl.ds(4 * PX + m, 8, stride=PX), :] = turned[0:8]
            dst[pl.ds(LAYERS * PX + m, 8, stride=PX), :] = turned[120:128]
        return c

    lax.fori_loop(0, PX, extract, 0, unroll=2)

    def phase2(up, field):
        ref, width = ((k_lab, W), (k_b, W - 1))[field]
        if up:
            src, dst = LAYERS + 8 - width, W - width
        else:
            src, dst = W, LAYERS + 8
        target = {"gz": jnp.clip(gz + (1 if up else -1), 0, gzn - 1)}
        return pltpu.make_async_remote_copy(
            src_ref=ref.at[pl.ds(src * PX, width * PX), :], dst_ref=ref.at[pl.ds(dst * PX, width * PX), :],
            send_sem=s2.at[up, field], recv_sem=r2.at[up, field], device_id=target, device_id_type=MESH)

    has = (gz > 0, gz < gzn - 1)
    for field in (0, 1):
        for up in (0, 1):
            @pl.when(has[up])
            def _():
                phase2(up, field).start()

    sub = lax.broadcasted_iota(jnp.int32, (8, 128), 0)
    lane = lax.broadcasted_iota(jnp.int32, (8, 128), 1)
    factor = (0.5, 0.5, 0.5, 0.25, 0.25, 0.25, 1.0)
    tables = []
    for c in range(7):
        tab = jnp.zeros((8, 128), jnp.float32)
        for label in range(8):
            tab = jnp.where(sub == label, cond[c, label], tab)
        tables.append(tab * factor[c])

    def lookup(lab):
        inside = lab < OUTSIDE
        index = jnp.bitwise_and(lab, 7)
        return [
            jnp.where(inside, jnp.take_along_axis(t, index, axis=0, mode="promise_in_bounds"), 0.0) for t in tables
        ], inside

    class Box:
        pass

    E, K = Box(), Box()
    E.ld = lambda ref, m, s: ref[m, pl.ds(s, 8), :]
    E.lab, E.b, E.inv = e_lab, e_b, e_inv
    E.sig = [e_sig.at[c] for c in range(7)]
    E.v = [e_v.at[k] for k in range(3)]
    E.tmp = [e_tmp.at[k] for k in range(5)]
    E.names = dict(m=0, s=1, l=2, ms=3, ml=4, sl=5)
    K.ld = lambda ref, m, s: ref[pl.ds(m * PX + s, 8), :]
    K.lab, K.b, K.inv = k_lab, k_b, k_inv
    K.sig = [k_sig.at[c] for c in range(7)]
    K.v = [k_v.at[k] for k in range(3)]
    K.tmp = [k_tmp.at[k] for k in range(5)]
    K.names = dict(m=2, s=0, l=1, ms=4, ml=5, sl=3)

    def e_st(ref, m, s, val):
        ref[m, pl.ds(s, 8), :] = val

    def k_st(ref, m, s, val):
        ref[pl.ds(m * PX + s, 8), :] = val

    E.st, K.st = e_st, k_st
    zero = jnp.zeros((8, 128), jnp.float32)
    left = lambda t: pltpu.roll(t, 127, 1)
    right = lambda t: pltpu.roll(t, 1, 1)

    def e_loop(halo, body, init):
        lo, count = W - halo, X + 2 * halo
        step = UNROLL

        def run(t, c):
            for u in range(step):
                c = body(lo + t * step + u, c)
            return c
        return lax.fori_loop(0, count // step, run, init)

    def k_loop(halo, body, init):
        def run(t, c):
            c = body(4 - halo + t, c)
            return body(LAYERS + 7 - halo + t, c)
        return lax.fori_loop(0, 2 * halo + 1, run, init)

    E.loop, K.loop = e_loop, k_loop
    E.span, K.span = Y, X
    E.inner = lambda m: (m >= W) & (m < W + X)
    K.inner = lambda m: (m == 4) | (m == LAYERS + 7)
    E.edge = (lane == 0) | (lane == 127)

    def insert(k, m, s, val):
        turned = pltpu.roll(kt[k, pl.ds(s, 8), :], lax.rem(255 - 2 * m, 128), 1)
        return jnp.where(E.edge, turned, val)

    E.insert = insert
    K.insert = lambda k, m, s, val: val

    def spans(box, halo):
        return group_spans(W - halo, W + box.span + halo, W, W + box.span)

    def masked(val, span, inner):
        start, low, high = span
        if low >= high:
            return None
        if (low, high) != (0, 8):
            val = jnp.where((sub >= low) & (sub < high), val, 0.0)
        return jnp.where(inner, val, 0.0)

    def stage_sigma(box, halo):
        def body(m, c):
            for s, _, _ in spans(box, W):
                sig, inside = lookup(box.ld(box.lab, m, s))
                for k in range(7):
                    box.st(box.sig[k], m, s, sig[k])
            return c
        box.loop(halo, body, 0)

    def stage_diag(box):
        nm = box.names
        sm, ss, sl = box.sig[nm["m"]], box.sig[nm["s"]], box.sig[nm["l"]]

        def body(m, acc):
            inner = box.inner(m)
            for span in spans(box, 3):
                s = span[0]
                cl = box.ld(sl, m, s)
                cm, cs = box.ld(sm, m, s), box.ld(ss, m, s)
                total = box.ld(box.sig[6], m, s) + 2.0 * (cl + cm + cs)
                total = total + box.ld(sm, m - 1, s) + box.ld(sm, m + 1, s)
                total = total + box.ld(ss, m, s - 1) + box.ld(ss, m, s + 1)
                total = total + left(cl) + right(cl)
                inv = jnp.where(box.ld(box.lab, m, s) < OUTSIDE, 1.0 / total, 0.0)
                b = box.ld(box.b, m, s)
                v0 = box.insert(0, m, s, b * inv)
                box.st(box.inv, m, s, inv)
                box.st(box.v[0], m, s, v0)
                part = masked(b * v0, span, inner)
                if part is not None:
                    acc = acc + part
            return acc
        return box.loop(3, body, zero)

    def stage_apply(box, k):
        nm = box.names
        v = box.v[k]
        sig = {name: box.sig[i] for name, i in nm.items()}
        t_ms, t_sl, t_s, t_d, t_z = box.tmp
        halo = 3 - k

        def first(m, c):
            for s, _, _ in spans(box, halo):
                val = box.ld(v, m, s)
                up, down = left(val), right(val)
                box.st(t_ms, m, s, box.ld(sig["ms"], m, s) * val)
                box.st(t_sl, m, s, box.ld(sig["sl"], m, s) * val)
                box.st(t_s, m, s, box.ld(sig["s"], m, s) * val)
                box.st(t_d, m, s, up - down)
                box.st(t_z, m, s, box.ld(sig["l"], m, s) * (up + down))
            return c
        box.loop(halo, first, 0)

        def second(m, accs):
            acc0, acc1 = accs
            inner = box.inner(m)
            for span in spans(box, halo - 1):
                s = span[0]
                ld = lambda ref, dm, ds: box.ld(ref, m + dm, s + ds)
                val = ld(v, 0, 0)
                hi, lo = ld(v, 1, 0), ld(v, -1, 0)
                g = ld(sig["m"], 0, 0) * (hi + lo)
                g = g + ld(sig["m"], 1, 0) * hi + ld(sig["m"], -1, 0) * lo
                cross = (ld(v, 1, 1) - ld(v, 1, -1)) - (ld(v, -1, 1) - ld(v, -1, -1))
                g = g + ld(sig["ms"], 0, 0) * cross
                g = g + ((ld(t_ms, 1, 1) - ld(t_ms, 1, -1)) - (ld(t_ms, -1, 1) - ld(t_ms, -1, -1)))
                g = g + ld(sig["s"], 0, 0) * (ld(v, 0, 1) + ld(v, 0, -1)) + (ld(t_s, 0, 1) + ld(t_s, 0, -1))
                g = g + ld(t_z, 0, 0)
                g = g + ld(sig["ml"], 0, 0) * (ld(t_d, 1, 0) - ld(t_d, -1, 0))
                g = g + ld(sig["sl"], 0, 0) * (ld(t_d, 0, 1) - ld(t_d, 0, -1))
                q = (ld(sig["ml"], 1, 0) * hi - ld(sig["ml"], -1, 0) * lo) + (ld(t_sl, 0, 1) - ld(t_sl, 0, -1))
                p = ld(sig["l"], 0, 0) * val
                g = g + left(p + q) + right(p - q)
                part = masked(val * g, span, inner)
                if part is not None:
                    acc0 = acc0 + part
                if k < 2:
                    nxt = box.insert(k + 1, m, s, g * ld(box.inv, 0, 0))
                    box.st(box.v[k + 1], m, s, nxt)
                    part = masked(nxt * g, span, inner)
                    if part is not None:
                        acc1 = acc1 + part
            return acc0, acc1
        return box.loop(halo - 1, second, (zero, zero))

    def stages(box):
        sums = [stage_diag(box)]
        for k in range(3):
            sums += stage_apply(box, k)
        return sums[:6]

    for field in (0, 1):
        for up in (0, 1):
            @pl.when(has[1 - up])
            def _():
                phase2(up, field).wait_recv()

    stage_sigma(K, 4)
    k_sums = stages(K)
    for k in range(3):
        kint[pl.ds(0, PX, stride=2), :] = k_v[k, pl.ds((LAYERS + 7) * PX, PX), :]
        kint[pl.ds(1, PX, stride=2), :] = k_v[k, pl.ds(4 * PX, PX), :]
        kt[k] = kint[...].T
    stage_sigma(E, 4)
    e_sums = stages(E)

    wide = lane[0:1]
    tile = zero
    for k in range(6):
        from_k = jnp.where((wide >= W) & (wide < W + Y), jnp.sum(k_sums[k], axis=0, keepdims=True), 0.0)
        from_e = jnp.where((wide > 0) & (wide < 127), jnp.sum(e_sums[k], axis=0, keepdims=True), 0.0)
        tile = jnp.where(sub == k, from_k + from_e, tile)

    stage = 0
    slot = 0
    for axis, pos, n in (("gy", gy, gyn), ("gx", gx, gxn), ("gz", gz, gzn)):
        ar[stage] = tile
        copies = []
        for d in range(1, n):
            copy = pltpu.make_async_remote_copy(
                src_ref=ar.at[stage], dst_ref=arslot.at[slot], send_sem=sa.at[slot], recv_sem=ra.at[slot],
                device_id={axis: lax.rem(pos + d, n)}, device_id_type=MESH)
            copy.start()
            copies.append((copy, slot))
            slot += 1
        for copy, where in copies:
            copy.wait_recv()
        for copy, where in copies:
            tile = tile + arslot[where]
        for copy, where in copies:
            copy.wait_send()
        stage += 1

    total = jnp.sum(tile, axis=1, keepdims=True)
    n = [jnp.broadcast_to(total[k:k + 1], (8, 128)) for k in range(6)]
    a = [n[k] - n[k + 1] for k in range(5)]
    safe = lambda num, den: jnp.where(den > 0, num / jnp.where(den > 0, den, 1.0), 0.0)
    l1, l2 = safe(a[1], a[0]), safe(a[2], a[0])
    d1 = a[2] - l1 * a[1]
    l21 = safe(a[3] - l1 * a[2], d1)
    d2 = a[4] - l2 * a[2] - l21 * (a[3] - l1 * a[2])
    y1 = n[1] - l1 * n[0]
    y2 = n[2] - l2 * n[0] - l21 * y1
    c2 = safe(y2, d2)
    c1 = safe(y1, d1) - l21 * c2
    c0 = safe(n[0], a[0]) - l1 * c1 - l2 * c2

    def finish(m, c):
        for s in range(0, Y, 8):
            out[m, pl.ds(s, 8), :] = (c0 * e_v[0, m + W, pl.ds(s + W, 8), :] + c1 * e_v[1, m + W, pl.ds(s + W, 8), :]
                                      + c2 * e_v[2, m + W, pl.ds(s + W, 8), :])
        return c

    lax.fori_loop(0, X, finish, 0, unroll=2)

    for field in (0, 1):
        for i, (dx, dy) in enumerate(DIRS):
            @pl.when(exists(dx, dy))
            def _():
                phase1(i, field).wait_send()
        for up in (0, 1):
            @pl.when(has[up])
            def _():
                phase2(up, field).wait_send()


def local(labels, conductivity, right_side, sizes):
    gxn, gyn, gzn = sizes
    X, Y, Z = labels.shape
    assert Z == 128 and Y % 8 == 0
    PX, PY = X + 2 * W, Y + 2 * W
    krows = 2 * LAYERS * PX
    f32 = jnp.float32
    slots = gxn + gyn + gzn - 3
    dma = pltpu.SemaphoreType.DMA
    return pl.pallas_call(
        functools.partial(kernel, (gxn, gyn, gzn, X, Y)),
        out_shape=jax.ShapeDtypeStruct((X, Y, Z), f32),
        in_specs=[
            pl.BlockSpec(memory_space=pltpu.SMEM),
            pl.BlockSpec(memory_space=pl.ANY),
            pl.BlockSpec(memory_space=pl.ANY),
        ],
        out_specs=pl.BlockSpec(memory_space=pltpu.VMEM),
        scratch_shapes=[
            pltpu.VMEM((PX, PY, 128), jnp.int32),
            pltpu.VMEM((PX, PY, 128), f32),
            pltpu.VMEM((7, PX, PY, 128), f32),
            pltpu.VMEM((PX, PY, 128), f32),
            pltpu.VMEM((3, PX, PY, 128), f32),
            pltpu.VMEM((5, PX, PY, 128), f32),
            pltpu.VMEM((krows, 128), jnp.int32),
            pltpu.VMEM((krows, 128), f32),
            pltpu.VMEM((7, krows, 128), f32),
            pltpu.VMEM((krows, 128), f32),
            pltpu.VMEM((3, krows, 128), f32),
            pltpu.VMEM((5, krows, 128), f32),
            pltpu.VMEM((128, 128), f32),
            pltpu.VMEM((3, 128, 128), f32),
            pltpu.VMEM((3, 8, 128), f32),
            pltpu.VMEM((slots, 8, 128), f32),
            dma((2,)), dma((8, 2)), dma((8, 2)), dma((2, 2)), dma((2, 2)), dma((slots,)), dma((slots,)),
        ],
        compiler_params=pltpu.CompilerParams(
            collective_id=0, has_side_effects=True, vmem_limit_bytes=62 * 1024 * 1024),
    )(conductivity, labels, right_side)


def solution(mesh):
    sizes = (mesh.shape["gx"], mesh.shape["gy"], mesh.shape["gz"])
    spec = P("gx", "gy", "gz")
    return jax.shard_map(
        functools.partial(local, sizes=sizes), mesh=mesh, in_specs=(spec, P(), spec), out_specs=spec, check_vma=False)
```

time: 384 us -> 58.2 us (0.15)
  other arithmetic: 109 us -> 0 us
  blocking collectives: 103 us -> 0 us
  local copies, waits for them, and re-layouts: 80.6 us -> 2.31 us
  starting transfers between devices: 58.6 us -> 0 us
  Pallas kernels: 0 us -> 55.8 us
  waiting for transfers between devices: 20.5 us -> 0 us
  between operations: 10.1 us -> 0.01 us
    psum x12 -> x0, blocking collectives: 103 us -> none  [by_axis(): return functools.reduce(lax.psum, axes, shard)]
    ppermute x24 -> x0, starting transfers between devices: 58.6 us -> none  [the longest x12 42.7 us: with_halo(): lax.ppermute(tail, axis, [(i, (i + 1) % count) for i in range(ends)])]
    pallas_call x0 -> x1, Pallas kernels: none -> 55.8 us  [local(): pl.pallas_call(functools.partial(kernel, (gxn, gyn, gzn, X, Y)), out_shap...]
    convert_element_type x8 -> x0, local copies, waits for them, and re-layouts: 28.8 us -> none  [lookup(): hit = (shifted == label + 1).astype(jnp.float32)]
    reduce_sum x4 -> x0, other arithmetic: 26.1 us -> none  [the longest x3 22.3 us: local(): jnp.sum(applied * precond)]
    concatenate x10 -> x0, other arithmetic: 23.5 us -> none  [with_halo(): jnp.concatenate([lax.ppermute(tail, axis, [(i, (i + 1) % count) for i in...]
    div x3 -> x0, other arithmetic: 22.8 us -> none  [the longest x1 12.8 us: local(): precond = residual / diag]
    add x3 -> x0, other arithmetic: 22 us -> none  [the longest x1 16.9 us: lookup(): total_flux + hit[None] * conductivity[:, label][:, None, None, None]]
  transfers between devices with their start and end apart: 24 -> 0, of which waited for: 9 -> 0; matrix products, arithmetic and copies ran while one was open for 6% -> 0% of each run, Pallas kernels for 0% -> 0%
where the time goes in v1:
time: 58.2 us; the launch traced here: 58.1 us
  Pallas kernels  55.8 us (96%)
  local copies, waits for them, and re-layouts  2.31 us (4%)
    pallas_call x1, Pallas kernels, local(): pl.pallas_call(functools.partial(kernel, (gxn, gyn, gzn, X, Y)), out_shap...  55.8 us
    unnamed x1, local copies, waits for them, and re-layouts  2.31 us

profile of v1, /device:TPU:0, one launch (start us, length us, event | category | flops | bytes accessed | tf_op | source)
XLA Modules:
  0.0 58.1 jit_solution(238214188653796208)
XLA Ops:
  0.0 55.8 %shard_map.37 = f32[32,64,128]{2,1,0:T(8,128)} custom-call(f32[7,8]{1,0:T(8,128)} %cond.1, s32[32,64,128]{2,1,0:T(8,128)} %lab_hbm.1, f32[32,64,128]{2,1,0:T(8,128)} %b_hbm.1), custom_call_target="tpu_custom_call" | custom-call | tf_op jit(solution)/shard_map/pallas_call | solution.py:428
  55.8 2.3 %copy.5 = f32[32,64,128]{2,1,0:T(8,128)} copy(f32[32,64,128]{2,1,0:T(8,128)} %shard_map.37) | data formatting | bytes 2097152

commit v2 on v1

v2 whole, which is shorter than its diff:
```python
import functools
import itertools
import math

import jax
import jax.numpy as jnp
from jax import lax
from jax.experimental import pallas as pl
from jax.experimental.pallas import tpu as pltpu
from jax.sharding import PartitionSpec as P

MESH = pl.DeviceIdType.MESH
W = 4
LAYERS = 12
OUTSIDE = 8
DIRS = tuple((a, b) for a in (-1, 0, 1) for b in (-1, 0, 1) if (a, b) != (0, 0))
STAGES = (("gx", "gy"), ("gz",))


def row_groups(lo, hi):
    starts = list(range(lo, hi - 7, 8))
    if starts[-1] + 8 < hi:
        starts.append(hi - 8)
    return starts


def group_spans(lo, hi, first, last):
    spans, done = [], first
    for start in row_groups(lo, hi):
        low, high = max(done, start), min(last, start + 8)
        done = max(done, high)
        spans.append((start, low - start, max(high, low) - start))
    return spans


def kernel(sizes, cond, lab_hbm, b_hbm, out, *scr):
    (gxn, gyn, gzn, X, Y) = sizes
    PX, PY = X + 2 * W, Y + 2 * W
    (e_lab, e_b, e_arr, k_lab, k_b, k_arr, kint, kt, ar, arslot,
     load_sem, s1, r1, s2, r2, sa, ra, greet) = scr
    gx, gy, gz = lax.axis_index("gx"), lax.axis_index("gy"), lax.axis_index("gz")

    load_lab = pltpu.make_async_copy(lab_hbm, e_lab.at[pl.ds(W, X), pl.ds(W, Y), :], load_sem.at[0])
    load_b = pltpu.make_async_copy(b_hbm, e_b.at[pl.ds(W, X), pl.ds(W, Y), :], load_sem.at[1])
    load_lab.start()
    load_b.start()

    def exists(dx, dy):
        ok = None
        for pos, d, n in ((gx, dx, gxn), (gy, dy, gyn)):
            if d:
                here = (pos + d >= 0) & (pos + d < n)
                ok = here if ok is None else ok & here
        return ok

    ring = {"gx": (gx, gxn), "gy": (gy, gyn), "gz": (gz, gzn)}

    def peers_of(axes):
        return [d for d in itertools.product(*[range(ring[a][1]) for a in axes]) if any(d)]

    def peer(axes, d):
        return {a: lax.rem(ring[a][0] + k, ring[a][1]) for a, k in zip(axes, d) if k}

    barrier = pltpu.get_barrier_semaphore()
    count = 0
    for axis in ("gy", "gx", "gz"):
        for d in peers_of((axis,)):
            pl.semaphore_signal(barrier, inc=1, device_id=peer((axis,), d), device_id_type=MESH)
            count = count + 1
    for dx, dy in DIRS:
        if dx and dy:
            ok = exists(dx, dy)

            @pl.when(ok)
            def _():
                pl.semaphore_signal(barrier, inc=1, device_id={"gx": gx + dx, "gy": gy + dy}, device_id_type=MESH)

            count = count + ok.astype(jnp.int32)
    pl.semaphore_wait(barrier, count)

    def pass_on(i, axis):
        for d in peers_of((axis,)):
            pl.semaphore_signal(greet.at[i], inc=1, device_id=peer((axis,), d), device_id_type=MESH)

    pass_on(0, "gx")

    def region(d, n, width, arriving):
        if d == 0:
            return pl.ds(W, n)
        if arriving:
            return pl.ds(W + n, width) if d < 0 else pl.ds(W - width, width)
        return pl.ds(W, width) if d < 0 else pl.ds(W + n - width, width)

    def phase1(i, field):
        dx, dy = DIRS[i]
        ref, width = ((e_lab, W), (e_b, W - 1))[field]
        src = ref.at[region(dx, X, width, False), region(dy, Y, width, False), :]
        dst = ref.at[region(dx, X, width, True), region(dy, Y, width, True), :]
        target = {}
        if dx:
            target["gx"] = jnp.clip(gx + dx, 0, gxn - 1)
        if dy:
            target["gy"] = jnp.clip(gy + dy, 0, gyn - 1)
        return pltpu.make_async_remote_copy(
            src_ref=src, dst_ref=dst, send_sem=s1.at[i, field], recv_sem=r1.at[i, field],
            device_id=target, device_id_type=MESH)

    for field, load in ((0, load_lab), (1, load_b)):
        load.wait()
        for i, (dx, dy) in enumerate(DIRS):
            @pl.when(exists(dx, dy))
            def _():
                phase1(i, field).start()

    def fill_e(xs, nx, ys, ny):
        def body(m, c):
            e_lab[xs + m, pl.ds(ys, ny), :] = jnp.full((ny, 128), OUTSIDE, jnp.int32)
            e_b[xs + m, pl.ds(ys, ny), :] = jnp.zeros((ny, 128), jnp.float32)
            return c
        lax.fori_loop(0, nx, body, 0)

    @pl.when(gx == 0)
    def _():
        fill_e(0, W, 0, PY)

    @pl.when(gx == gxn - 1)
    def _():
        fill_e(W + X, W, 0, PY)

    @pl.when(gy == 0)
    def _():
        fill_e(0, PX, 0, W)

    @pl.when(gy == gyn - 1)
    def _():
        fill_e(0, PX, W + Y, W)

    def fill_k(side, layer):
        rows = pl.ds((side * LAYERS + layer) * PX, W * PX)
        k_lab[rows, :] = jnp.full((W * PX, 128), OUTSIDE, jnp.int32)
        k_b[rows, :] = jnp.zeros((W * PX, 128), jnp.float32)

    @pl.when(gz == 0)
    def _():
        fill_k(0, 0)

    @pl.when(gz == gzn - 1)
    def _():
        fill_k(1, 2 * W)

    def arrive(pick):
        for field in (0, 1):
            for i, (dx, dy) in enumerate(DIRS):
                if pick(dx, dy):
                    @pl.when(exists(-dx, -dy))
                    def _():
                        phase1(i, field).wait_recv()

    def phase2(up, field):
        ref, width = ((k_lab, W), (k_b, W - 1))[field]
        if up:
            src, dst = LAYERS + 8 - width, W - width
        else:
            src, dst = W, LAYERS + 8
        target = {"gz": jnp.clip(gz + (1 if up else -1), 0, gzn - 1)}
        return pltpu.make_async_remote_copy(
            src_ref=ref.at[pl.ds(src * PX, width * PX), :], dst_ref=ref.at[pl.ds(dst * PX, width * PX), :],
            send_sem=s2.at[up, field], recv_sem=r2.at[up, field], device_id=target, device_id_type=MESH)

    has = (gz > 0, gz < gzn - 1)

    sub = lax.broadcasted_iota(jnp.int32, (8, 128), 0)
    lane = lax.broadcasted_iota(jnp.int32, (8, 128), 1)
    factor = (0.5, 0.5, 0.5, 0.25, 0.25, 0.25, 1.0)
    tables = []
    for c in range(7):
        tab = jnp.zeros((8, 128), jnp.float32)
        for label in range(8):
            tab = jnp.where(sub == label, cond[c, label], tab)
        tables.append(tab * factor[c])

    def lookup(lab):
        inside = lab < OUTSIDE
        index = jnp.bitwise_and(lab, 7)
        return [
            jnp.where(inside, jnp.take_along_axis(t, index, axis=0, mode="promise_in_bounds"), 0.0) for t in tables
        ], inside

    class Box:
        pass

    E, K = Box(), Box()
    E.at = lambda m, s: (m, pl.ds(s, 8), slice(None))
    K.at = lambda m, s: (pl.ds(m * PX + s, 8), slice(None))
    for box, lab, rhs, arrays in ((E, e_lab, e_b, e_arr), (K, k_lab, k_b, k_arr)):
        box.lab, box.b = lab, rhs
        box.sig = [arrays.at[c] for c in range(7)]
        box.fm, box.fs, box.fl, box.fr, box.cpp, box.cpm, box.inv = [arrays.at[7 + c] for c in range(7)]
        box.v = [arrays.at[14 + c] for c in range(3)]
        ping, pong = (arrays.at[17], arrays.at[18]), (arrays.at[19], arrays.at[20])
        box.t = [ping, pong, ping]
    E.names, K.names = (0, 1, 2, 3, 4, 5), (2, 0, 1, 4, 5, 3)
    E.span, K.span = Y, X
    E.inner = lambda m: (m >= W) & (m < W + X)
    zero = jnp.zeros((8, 128), jnp.float32)
    left = lambda t: pltpu.roll(t, 127, 1)
    right = lambda t: pltpu.roll(t, 1, 1)

    class Cells:
        def __init__(self, box, m):
            self.box, self.m, self.seen = box, m, {}

        def __call__(self, ref, dm, s):
            key = (id(ref), dm, s)
            if key not in self.seen:
                self.seen[key] = ref[self.box.at(self.m + dm, s)]
            return self.seen[key]

    def run(loop, body, init):
        base, stride, trips, _ = loop
        return lax.fori_loop(0, trips, lambda t, c: body(base + t * stride, c), init)

    def spans(box, halo):
        return group_spans(W - halo, W + box.span + halo, W, W + box.span)

    def clip(val, span):
        _, low, high = span
        if low >= high:
            return None
        if (low, high) != (0, 8):
            val = jnp.where((sub >= low) & (sub < high), val, 0.0)
        return val

    def add(total, val):
        return val if total is None else total if val is None else total + val

    def gather(box, m, acc, parts, inner):
        for u, part in enumerate(parts):
            if part is not None and (inner is None or inner == "ask" or u in inner):
                acc = acc + (jnp.where(box.inner(m + u), part, 0.0) if inner == "ask" else part)
        return acc

    def sigma(box, loop, starts):
        def body(m, c):
            for s in starts:
                for u in range(loop[3]):
                    sig, _ = lookup(box.lab[box.at(m + u, s)])
                    for k in range(7):
                        box.sig[k][box.at(m + u, s)] = sig[k]
            return c
        run(loop, body, 0)

    def spread(box, m, s, v, fl, fr):
        up, down = left(v), right(v)
        box.t[0][0][box.at(m, s)] = up - down
        box.t[0][1][box.at(m, s)] = fl * up + fr * down

    def diagonal(box, loop, inner, acc):
        sm, ss, sl, ms = [box.sig[box.names[i]] for i in range(4)]

        def body(m, acc):
            ld = Cells(box, m)
            parts = [None] * loop[3]
            for span in spans(box, 3):
                s = span[0]
                for u in range(loop[3]):
                    at = box.at(m + u, s)
                    cm, cs, cl, cx = ld(sm, u, s), ld(ss, u, s), ld(sl, u, s), ld(ms, u, s)
                    fm, fs = cm + ld(sm, u + 1, s), cs + ld(ss, u, s + 1)
                    fl, fr = cl + left(cl), cl + right(cl)
                    total = (ld(box.sig[6], u, s) + fm + (cm + ld(sm, u - 1, s))) + (fs + (cs + ld(ss, u, s - 1)))
                    total = total + (fl + fr)
                    inv = jnp.where(ld(box.lab, u, s) < OUTSIDE, 1.0 / total, 0.0)
                    b = ld(box.b, u, s)
                    v0 = b * inv
                    box.fm[at], box.fs[at], box.fl[at], box.fr[at] = fm, fs, fl, fr
                    box.cpp[at] = cx + ld(ms, u + 1, s + 1)
                    box.cpm[at] = -(cx + ld(ms, u + 1, s - 1))
                    box.inv[at] = inv
                    box.v[0][at] = v0
                    spread(box, m + u, s, v0, fl, fr)
                    parts[u] = add(parts[u], clip(b * v0, span))
            return gather(box, m, acc, parts, inner)
        return run(loop, body, acc)

    def apply(box, k, loop, inner, accs):
        v, ml, sl = box.v[k], box.sig[box.names[4]], box.sig[box.names[5]]

        def body(m, accs):
            ld = Cells(box, m)
            nxt_td = {}
            parts0, parts1 = [None] * loop[3], [None] * loop[3]
            for span in spans(box, 2 - k):
                s = span[0]
                for u in range(loop[3]):
                    at = box.at(m + u, s)
                    val, hi, lo = ld(v, u, s), ld(v, u + 1, s), ld(v, u - 1, s)
                    up, down = ld(v, u, s + 1), ld(v, u, s - 1)
                    a1 = ld(box.fm, u, s) * hi + ld(box.fm, u - 1, s) * lo
                    a2 = ld(box.fs, u, s) * up + ld(box.fs, u, s - 1) * down
                    a3 = ld(box.cpp, u, s) * ld(v, u + 1, s + 1) + ld(box.cpp, u - 1, s - 1) * ld(v, u - 1, s - 1)
                    a4 = ld(box.cpm, u, s) * ld(v, u + 1, s - 1) + ld(box.cpm, u - 1, s + 1) * ld(v, u - 1, s + 1)
                    q = (ld(ml, u + 1, s) * hi - ld(ml, u - 1, s) * lo) + (
                        ld(sl, u, s + 1) * up - ld(sl, u, s - 1) * down)
                    a5 = ld(ml, u, s) * (ld(tin, u + 1, s) - ld(tin, u - 1, s))
                    a6 = ld(sl, u, s) * (ld(tin, u, s + 1) - ld(tin, u, s - 1))
                    g = ((a1 + a2) + (a3 + a4)) + ((a5 + a6) + ld(zin, u, s)) + (left(q) - right(q))
                    parts0[u] = add(parts0[u], clip(val * g, span))
                    if k < 2:
                        nxt = g * ld(box.inv, u, s)
                        box.v[k + 1][at] = nxt
                        up, down = left(nxt), right(nxt)
                        tout[at] = up - down
                        zout[at] = ld(box.fl, u, s) * up + ld(box.fr, u, s) * down
                        parts1[u] = add(parts1[u], clip(nxt * g, span))
            acc0, acc1 = accs
            return gather(box, m, acc0, parts0, inner), gather(box, m, acc1, parts1, inner)

        tin, zin, tout, zout = box.t[k] + (box.t[k + 1] if k < 2 else (None, None))
        return run(loop, body, accs)

    def extract(base, count, unroll):
        def body(m, c):
            for src, dst in ((e_lab, k_lab), (e_b, k_b)):
                plane = jnp.concatenate([src[base + m], jnp.zeros((128 - PY, 128), src.dtype)], axis=0)
                turned = plane.T
                dst[pl.ds(4 * PX + base + m, 8, stride=PX), :] = turned[0:8]
                dst[pl.ds(LAYERS * PX + base + m, 8, stride=PX), :] = turned[120:128]
            return c
        lax.fori_loop(0, count, body, 0, unroll=unroll)

    own_rows = [W + 8 * i for i in range(Y // 8)]
    sigma(E, (W, 4, X // 4, 4), own_rows)
    arrive(lambda dx, dy: dx == 0)
    sigma(E, (W, 4, X // 4, 4), [0, PY - 8])
    extract(W, X, 4)
    s0 = diagonal(E, (W + 1, 3, (X - 2) // 3, 3), None, zero)
    s12 = apply(E, 0, (W + 2, 4, (X - 4) // 4, 4), None, (zero, zero))

    arrive(lambda dx, dy: dx != 0)
    extract(0, W, 4)
    extract(W + X, W, 4)
    sigma(E, (0, X + W, 2, 4), row_groups(0, PY))
    for field in (0, 1):
        for up in (0, 1):
            @pl.when(has[up])
            def _():
                phase2(up, field).start()

    s0 = diagonal(E, (1, X + 2, 2, 4), "ask", s0)
    s12 = apply(E, 0, (2, X, 2, 4), "ask", s12)
    s34 = apply(E, 1, (2, 4, (X + 4) // 4, 4), "ask", (zero, zero))
    s5, _ = apply(E, 2, (W, 4, X // 4, 4), None, (zero, zero))
    e_sums = [s0, *s12, *s34, s5]

    for field in (0, 1):
        for up in (0, 1):
            @pl.when(has[1 - up])
            def _():
                phase2(up, field).wait_recv()
    sigma(K, (0, 4, LAYERS // 2, 4), row_groups(0, PX))
    s0 = diagonal(K, (1, LAYERS, 2, 10), (3, 4, 5, 6), zero)
    s12 = apply(K, 0, (2, LAYERS, 2, 8), (2, 3, 4, 5), (zero, zero))
    s34 = apply(K, 1, (3, LAYERS, 2, 6), (1, 2, 3, 4), (zero, zero))
    s5, _ = apply(K, 2, (4, LAYERS, 2, 4), None, (zero, zero))
    k_sums = [s0, *s12, *s34, s5]

    edge = (lane < 4) | (lane >= 124)
    blocks = -(-X // 16)

    def complete():
        for k in range(3):
            for j in range(4):
                kint[pl.ds(j, X, stride=8), :] = K.v[k][pl.ds((LAYERS + 4 + j) * PX + W, X), :]
                kint[pl.ds(4 + j, X, stride=8), :] = K.v[k][pl.ds((4 + j) * PX + W, X), :]
            for q in range(blocks):
                kt[k, q] = kint[128 * q:128 * q + 128, :].T

        def body(m, c):
            for k in range(3):
                for s in range(W, W + Y, 8):
                    turned = pltpu.roll(kt[k, m // 16, pl.ds(s, 8), :], lax.rem(252 - 8 * lax.rem(m, 16), 128), 1)
                    E.v[k][m + W, pl.ds(s, 8), :] = jnp.where(edge, turned, E.v[k][m + W, pl.ds(s, 8), :])
            return c
        lax.fori_loop(0, X, body, 0, unroll=2)

    wide = lane[0:1]
    row = jnp.zeros((1, 128), jnp.float32)
    for k in range(6):
        from_k = jnp.where((wide >= W) & (wide < W + Y), jnp.sum(k_sums[k], axis=0, keepdims=True), 0.0)
        from_e = jnp.where((wide >= 4) & (wide < 124), jnp.sum(e_sums[k], axis=0, keepdims=True), 0.0)
        row = jnp.where(wide == k, jnp.sum(from_k + from_e, axis=1, keepdims=True), row)

    pl.semaphore_wait(greet.at[0], gxn - 1)
    slot = 0
    for stage, axes in enumerate(STAGES):
        ar[stage] = jnp.broadcast_to(row, (8, 128))
        copies = []
        first = slot
        for d in peers_of(axes):
            copy = pltpu.make_async_remote_copy(
                src_ref=ar.at[stage, pl.ds(0, 1), :], dst_ref=arslot.at[pl.ds(slot, 1), :], send_sem=sa.at[slot],
                recv_sem=ra.at[slot], device_id=peer(axes, d), device_id_type=MESH)
            copy.start()
            copies.append(copy)
            slot += 1
        if stage == 0:
            complete()
        for copy in copies:
            copy.wait_recv()
        row = row + jnp.sum(arslot[first:slot, :], axis=0, keepdims=True)
        for copy in copies:
            copy.wait_send()

    n = [jnp.broadcast_to(row[:, k:k + 1], (8, 128)) for k in range(6)]
    a = [n[k] - n[k + 1] for k in range(5)]
    safe = lambda num, den: jnp.where(den > 0, num / jnp.where(den > 0, den, 1.0), 0.0)
    l1, l2 = safe(a[1], a[0]), safe(a[2], a[0])
    d1 = a[2] - l1 * a[1]
    l21 = safe(a[3] - l1 * a[2], d1)
    d2 = a[4] - l2 * a[2] - l21 * (a[3] - l1 * a[2])
    y1 = n[1] - l1 * n[0]
    y2 = n[2] - l2 * n[0] - l21 * y1
    c2 = safe(y2, d2)
    c1 = safe(y1, d1) - l21 * c2
    c0 = safe(n[0], a[0]) - l1 * c1 - l2 * c2

    def finish(m, c):
        for s in range(0, Y, 8):
            out[m, pl.ds(s, 8), :] = (c0 * E.v[0][m + W, pl.ds(s + W, 8), :] + c1 * E.v[1][m + W, pl.ds(s + W, 8), :]
                                      + c2 * E.v[2][m + W, pl.ds(s + W, 8), :])
        return c

    lax.fori_loop(0, X, finish, 0, unroll=2)

    for field in (0, 1):
        for i, (dx, dy) in enumerate(DIRS):
            @pl.when(exists(dx, dy))
            def _():
                phase1(i, field).wait_send()
        for up in (0, 1):
            @pl.when(has[up])
            def _():
                phase2(up, field).wait_send()


def local(labels, conductivity, right_side, sizes):
    gxn, gyn, gzn = sizes
    X, Y, Z = labels.shape
    assert Z == 128 and Y % 8 == 0
    PX, PY = X + 2 * W, Y + 2 * W
    krows = 2 * LAYERS * PX
    f32 = jnp.float32
    count = {"gx": gxn, "gy": gyn, "gz": gzn}
    slots = sum(math.prod(count[a] for a in axes) - 1 for axes in STAGES)
    dma = pltpu.SemaphoreType.DMA
    return pl.pallas_call(
        functools.partial(kernel, (gxn, gyn, gzn, X, Y)),
        out_shape=jax.ShapeDtypeStruct((X, Y, Z), f32),
        in_specs=[
            pl.BlockSpec(memory_space=pltpu.SMEM),
            pl.BlockSpec(memory_space=pl.ANY),
            pl.BlockSpec(memory_space=pl.ANY),
        ],
        out_specs=pl.BlockSpec(memory_space=pltpu.VMEM),
        scratch_shapes=[
            pltpu.VMEM((PX, PY, 128), jnp.int32),
            pltpu.VMEM((PX, PY, 128), f32),
            pltpu.VMEM((21, PX, PY, 128), f32),
            pltpu.VMEM((krows, 128), jnp.int32),
            pltpu.VMEM((krows, 128), f32),
            pltpu.VMEM((21, krows, 128), f32),
            pltpu.VMEM((-(-X // 16) * 128, 128), f32),
            pltpu.VMEM((3, -(-X // 16), 128, 128), f32),
            pltpu.VMEM((3, 8, 128), f32),
            pltpu.VMEM((slots, 128), f32),
            dma((2,)), dma((8, 2)), dma((8, 2)), dma((2, 2)), dma((2, 2)), dma((slots,)), dma((slots,)),
            pltpu.SemaphoreType.REGULAR((2,)),
        ],
        compiler_params=pltpu.CompilerParams(
            collective_id=0, has_side_effects=True, vmem_limit_bytes=62 * 1024 * 1024),
    )(conductivity, labels, right_side)


def solution(mesh):
    sizes = (mesh.shape["gx"], mesh.shape["gy"], mesh.shape["gz"])
    spec = P("gx", "gy", "gz")
    return jax.shard_map(
        functools.partial(local, sizes=sizes), mesh=mesh, in_specs=(spec, P(), spec), out_specs=spec, check_vma=False)
```

time: 58.2 us -> 41.3 us (0.71)
  Pallas kernels: 55.8 us -> 38.8 us
    pallas_call x1, Pallas kernels: 55.8 us -> 38.8 us  [local(): pl.pallas_call(functools.partial(kernel, (gxn, gyn, gzn, X, Y)), out_shap...]
where the time goes in v2:
time: 41.3 us; the launch traced here: 41.1 us
  Pallas kernels  38.8 us (94%)
  local copies, waits for them, and re-layouts  2.31 us (6%)
    pallas_call x1, Pallas kernels, local(): pl.pallas_call(functools.partial(kernel, (gxn, gyn, gzn, X, Y)), out_shap...  38.8 us
    unnamed x1, local copies, waits for them, and re-layouts  2.31 us

profile of v2, /device:TPU:0, one launch (start us, length us, event | category | flops | bytes accessed | tf_op | source)
XLA Modules:
  0.0 41.1 jit_solution(904367986433119319)
XLA Ops:
  0.0 38.8 %shard_map.37 = f32[32,64,128]{2,1,0:T(8,128)} custom-call(f32[7,8]{1,0:T(8,128)} %cond.1, s32[32,64,128]{2,1,0:T(8,128)} %lab_hbm.1, f32[32,64,128]{2,1,0:T(8,128)} %b_hbm.1), custom_call_target="tpu_custom_call" | custom-call | tf_op jit(solution)/shard_map/pallas_call | solution.py:457
  38.8 2.3 %copy.5 = f32[32,64,128]{2,1,0:T(8,128)} copy(f32[32,64,128]{2,1,0:T(8,128)} %shard_map.37) | data formatting | bytes 2097152

commit v3 on v2

--- a/solution.py
+++ b/solution.py
@@ -12,8 +12,9 @@
 MESH = pl.DeviceIdType.MESH
 W = 4
 LAYERS = 12
+SKEW = 8
 OUTSIDE = 8
-DIRS = tuple((a, b) for a in (-1, 0, 1) for b in (-1, 0, 1) if (a, b) != (0, 0))
+DIRS = ((0, -1), (0, 1), (-1, 0), (1, 0), (-1, -1), (-1, 1), (1, -1), (1, 1))
 STAGES = (("gx", "gy"), ("gz",))
 
 
@@ -33,15 +34,18 @@
     return spans
 
 
-def kernel(sizes, cond, lab_hbm, b_hbm, out, *scr):
+def kernel(sizes, cond_hbm, lab_hbm, b_hbm, out_any, *scr):
     (gxn, gyn, gzn, X, Y) = sizes
     PX, PY = X + 2 * W, Y + 2 * W
+    KX = PX + 1
     (e_lab, e_b, e_arr, k_lab, k_b, k_arr, kint, kt, ar, arslot,
-     load_sem, s1, r1, s2, r2, sa, ra, greet) = scr
+     load_sem, s1, r1, s2, r2, sa, ra, greet, out, out_sem, cond) = scr
     gx, gy, gz = lax.axis_index("gx"), lax.axis_index("gy"), lax.axis_index("gz")
 
     load_lab = pltpu.make_async_copy(lab_hbm, e_lab.at[pl.ds(W, X), pl.ds(W, Y), :], load_sem.at[0])
     load_b = pltpu.make_async_copy(b_hbm, e_b.at[pl.ds(W, X), pl.ds(W, Y), :], load_sem.at[1])
+    load_cond = pltpu.make_async_copy(cond_hbm, cond, load_sem.at[2])
+    load_cond.start()
     load_lab.start()
     load_b.start()
 
@@ -136,9 +140,9 @@
         fill_e(0, PX, W + Y, W)
 
     def fill_k(side, layer):
-        rows = pl.ds((side * LAYERS + layer) * PX, W * PX)
-        k_lab[rows, :] = jnp.full((W * PX, 128), OUTSIDE, jnp.int32)
-        k_b[rows, :] = jnp.zeros((W * PX, 128), jnp.float32)
+        rows = pl.ds((side * LAYERS + layer) * KX, W * KX)
+        k_lab[rows, :] = jnp.full((W * KX, 128), OUTSIDE, jnp.int32)
+        k_b[rows, :] = jnp.zeros((W * KX, 128), jnp.float32)
 
     @pl.when(gz == 0)
     def _():
@@ -164,11 +168,12 @@
             src, dst = W, LAYERS + 8
         target = {"gz": jnp.clip(gz + (1 if up else -1), 0, gzn - 1)}
         return pltpu.make_async_remote_copy(
-            src_ref=ref.at[pl.ds(src * PX, width * PX), :], dst_ref=ref.at[pl.ds(dst * PX, width * PX), :],
+            src_ref=ref.at[pl.ds(src * KX, width * KX), :], dst_ref=ref.at[pl.ds(dst * KX, width * KX), :],
             send_sem=s2.at[up, field], recv_sem=r2.at[up, field], device_id=target, device_id_type=MESH)
 
     has = (gz > 0, gz < gzn - 1)
 
+    load_cond.wait()
     sub = lax.broadcasted_iota(jnp.int32, (8, 128), 0)
     lane = lax.broadcasted_iota(jnp.int32, (8, 128), 1)
     factor = (0.5, 0.5, 0.5, 0.25, 0.25, 0.25, 1.0)
@@ -179,28 +184,46 @@
             tab = jnp.where(sub == label, cond[c, label], tab)
         tables.append(tab * factor[c])
 
-    def lookup(lab):
+    def lookup(lab, picks):
         inside = lab < OUTSIDE
         index = jnp.bitwise_and(lab, 7)
-        return [
-            jnp.where(inside, jnp.take_along_axis(t, index, axis=0, mode="promise_in_bounds"), 0.0) for t in tables
-        ], inside
+        return [jnp.where(inside, jnp.take_along_axis(tables[k], index, axis=0, mode="promise_in_bounds"), 0.0)
+                for k in picks]
 
     class Box:
         pass
 
+    class Field:
+        def __init__(self, ref, base, height):
+            self.ref, self.base, self.height = ref, base, height
+
+        def rows(self, m, s, n=8):
+            return pl.ds(self.base + m * self.height + s, n), slice(None)
+
+        def __getitem__(self, at):
+            return self.ref[self.rows(*at)]
+
+        def __setitem__(self, at, val):
+            self.ref[self.rows(*at)] = val
+
+    class Block(Field):
+        def rows(self, m, s):
+            return m, pl.ds(s, 8), slice(None)
+
     E, K = Box(), Box()
-    E.at = lambda m, s: (m, pl.ds(s, 8), slice(None))
-    K.at = lambda m, s: (pl.ds(m * PX + s, 8), slice(None))
-    for box, lab, rhs, arrays in ((E, e_lab, e_b, e_arr), (K, k_lab, k_b, k_arr)):
-        box.lab, box.b = lab, rhs
-        box.sig = [arrays.at[c] for c in range(7)]
-        box.fm, box.fs, box.fl, box.fr, box.cpp, box.cpm, box.inv = [arrays.at[7 + c] for c in range(7)]
-        box.v = [arrays.at[14 + c] for c in range(3)]
-        ping, pong = (arrays.at[17], arrays.at[18]), (arrays.at[19], arrays.at[20])
-        box.t = [ping, pong, ping]
+    E.lab, E.b = Block(e_lab, 0, PY), Block(e_b, 0, PY)
+    K.lab, K.b = Field(k_lab, 0, KX), Field(k_b, 0, KX)
+    E.arrays = [Field(e_arr, c * (PX * PY + SKEW), PY) for c in range(18)]
+    K.arrays = [Field(k_arr, c * (2 * LAYERS * KX + SKEW), KX) for c in range(18)]
+    for box in (E, K):
+        a = box.arrays
+        box.sig = a[:6]
+        box.fm, box.fs, box.cpp, box.cpm, box.inv = a[6:11]
+        box.v = a[11:14]
+        box.t = [(a[14], a[15]), (a[16], a[17]), (a[14], a[15])]
     E.names, K.names = (0, 1, 2, 3, 4, 5), (2, 0, 1, 4, 5, 3)
     E.span, K.span = Y, X
+    K.inner = lambda m: ((m >= 4) & (m < 8)) | ((m >= LAYERS + 4) & (m < LAYERS + 8))
     E.inner = lambda m: (m >= W) & (m < W + X)
     zero = jnp.zeros((8, 128), jnp.float32)
     left = lambda t: pltpu.roll(t, 127, 1)
@@ -213,12 +236,13 @@
         def __call__(self, ref, dm, s):
             key = (id(ref), dm, s)
             if key not in self.seen:
-                self.seen[key] = ref[self.box.at(self.m + dm, s)]
+                self.seen[key] = ref[self.m + dm, s]
             return self.seen[key]
 
     def run(loop, body, init):
         base, stride, trips, _ = loop
-        return lax.fori_loop(0, trips, lambda t, c: body(base + t * stride, c), init)
+        start = base if callable(base) else lambda t: base + t * stride
+        return lax.fori_loop(0, trips, lambda t, c: body(start(t), c), init)
 
     def spans(box, halo):
         return group_spans(W - halo, W + box.span + halo, W, W + box.span)
@@ -244,16 +268,16 @@
         def body(m, c):
             for s in starts:
                 for u in range(loop[3]):
-                    sig, _ = lookup(box.lab[box.at(m + u, s)])
-                    for k in range(7):
-                        box.sig[k][box.at(m + u, s)] = sig[k]
+                    sig = lookup(box.lab[m + u, s], range(6))
+                    for k in range(6):
+                        box.sig[k][m + u, s] = sig[k]
             return c
         run(loop, body, 0)
 
-    def spread(box, m, s, v, fl, fr):
+    def spread(box, k, m, s, v):
         up, down = left(v), right(v)
-        box.t[0][0][box.at(m, s)] = up - down
-        box.t[0][1][box.at(m, s)] = fl * up + fr * down
+        box.t[k][0][m, s] = up - down
+        box.t[k][1][m, s] = up + down
 
     def diagonal(box, loop, inner, acc):
         sm, ss, sl, ms = [box.sig[box.names[i]] for i in range(4)]
@@ -264,36 +288,35 @@
             for span in spans(box, 3):
                 s = span[0]
                 for u in range(loop[3]):
-                    at = box.at(m + u, s)
+                    at = (m + u, s)
                     cm, cs, cl, cx = ld(sm, u, s), ld(ss, u, s), ld(sl, u, s), ld(ms, u, s)
                     fm, fs = cm + ld(sm, u + 1, s), cs + ld(ss, u, s + 1)
-                    fl, fr = cl + left(cl), cl + right(cl)
-                    total = (ld(box.sig[6], u, s) + fm + (cm + ld(sm, u - 1, s))) + (fs + (cs + ld(ss, u, s - 1)))
-                    total = total + (fl + fr)
-                    inv = jnp.where(ld(box.lab, u, s) < OUTSIDE, 1.0 / total, 0.0)
+                    lab = ld(box.lab, u, s)
+                    total = (lookup(lab, (6,))[0] + fm + (cm + ld(sm, u - 1, s))) + (fs + (cs + ld(ss, u, s - 1)))
+                    total = total + ((cl + cl) + (left(cl) + right(cl)))
+                    inv = jnp.where(lab < OUTSIDE, 1.0 / total, 0.0)
                     b = ld(box.b, u, s)
                     v0 = b * inv
-                    box.fm[at], box.fs[at], box.fl[at], box.fr[at] = fm, fs, fl, fr
+                    box.fm[at], box.fs[at] = fm, fs
                     box.cpp[at] = cx + ld(ms, u + 1, s + 1)
                     box.cpm[at] = -(cx + ld(ms, u + 1, s - 1))
                     box.inv[at] = inv
                     box.v[0][at] = v0
-                    spread(box, m + u, s, v0, fl, fr)
+                    spread(box, 0, m + u, s, v0)
                     parts[u] = add(parts[u], clip(b * v0, span))
             return gather(box, m, acc, parts, inner)
         return run(loop, body, acc)
 
     def apply(box, k, loop, inner, accs):
-        v, ml, sl = box.v[k], box.sig[box.names[4]], box.sig[box.names[5]]
+        v, lx, ml, sl = box.v[k], box.sig[box.names[2]], box.sig[box.names[4]], box.sig[box.names[5]]
 
         def body(m, accs):
             ld = Cells(box, m)
-            nxt_td = {}
             parts0, parts1 = [None] * loop[3], [None] * loop[3]
             for span in spans(box, 2 - k):
                 s = span[0]
                 for u in range(loop[3]):
-                    at = box.at(m + u, s)
+                    at = (m + u, s)
                     val, hi, lo = ld(v, u, s), ld(v, u + 1, s), ld(v, u - 1, s)
                     up, down = ld(v, u, s + 1), ld(v, u, s - 1)
                     a1 = ld(box.fm, u, s) * hi + ld(box.fm, u - 1, s) * lo
@@ -304,42 +327,51 @@
                         ld(sl, u, s + 1) * up - ld(sl, u, s - 1) * down)
                     a5 = ld(ml, u, s) * (ld(tin, u + 1, s) - ld(tin, u - 1, s))
                     a6 = ld(sl, u, s) * (ld(tin, u, s + 1) - ld(tin, u, s - 1))
-                    g = ((a1 + a2) + (a3 + a4)) + ((a5 + a6) + ld(zin, u, s)) + (left(q) - right(q))
+                    c = ld(lx, u, s)
+                    p = c * val
+                    g = ((a1 + a2) + (a3 + a4)) + ((a5 + a6) + c * ld(zin, u, s)) + (left(p + q) + right(p - q))
                     parts0[u] = add(parts0[u], clip(val * g, span))
                     if k < 2:
                         nxt = g * ld(box.inv, u, s)
                         box.v[k + 1][at] = nxt
-                        up, down = left(nxt), right(nxt)
-                        tout[at] = up - down
-                        zout[at] = ld(box.fl, u, s) * up + ld(box.fr, u, s) * down
+                        spread(box, k + 1, m + u, s, nxt)
                         parts1[u] = add(parts1[u], clip(nxt * g, span))
             acc0, acc1 = accs
             return gather(box, m, acc0, parts0, inner), gather(box, m, acc1, parts1, inner)
 
-        tin, zin, tout, zout = box.t[k] + (box.t[k + 1] if k < 2 else (None, None))
+        tin, zin = box.t[k]
         return run(loop, body, accs)
 
-    def extract(base, count, unroll):
-        def body(m, c):
-            for src, dst in ((e_lab, k_lab), (e_b, k_b)):
-                plane = jnp.concatenate([src[base + m], jnp.zeros((128 - PY, 128), src.dtype)], axis=0)
-                turned = plane.T
-                dst[pl.ds(4 * PX + base + m, 8, stride=PX), :] = turned[0:8]
-                dst[pl.ds(LAYERS * PX + base + m, 8, stride=PX), :] = turned[120:128]
+    def extract(plane, trips):
+        mine = [jnp.right_shift(lane, 4) == p for p in range(8)]
+
+        def body(t, c):
+            for src, dst in ((E.lab, k_lab), (E.b, k_b)):
+                tiles = []
+                for s in range(0, PY, 8):
+                    tile = pltpu.roll(src[plane(t, 0), s], 8, 1)
+                    for p in range(1, 8):
+                        tile = jnp.where(mine[p], pltpu.roll(src[plane(t, p), s], (8 + 16 * p) % 128, 1), tile)
+                    tiles.append(tile)
+                tiles.append(jnp.zeros((128 - PY, 128), tile.dtype))
+                turned = jnp.concatenate(tiles, axis=0).T
+                for p in range(8):
+                    x = plane(t, p)
+                    dst[pl.ds(LAYERS * KX + x, 8, stride=KX), :] = turned[16 * p:16 * p + 8]
+                    dst[pl.ds(4 * KX + x, 8, stride=KX), :] = turned[16 * p + 8:16 * p + 16]
             return c
-        lax.fori_loop(0, count, body, 0, unroll=unroll)
+        lax.fori_loop(0, trips, body, 0)
 
     own_rows = [W + 8 * i for i in range(Y // 8)]
     sigma(E, (W, 4, X // 4, 4), own_rows)
     arrive(lambda dx, dy: dx == 0)
     sigma(E, (W, 4, X // 4, 4), [0, PY - 8])
-    extract(W, X, 4)
+    extract(lambda t, p: W + 8 * t + p, X // 8)
     s0 = diagonal(E, (W + 1, 3, (X - 2) // 3, 3), None, zero)
     s12 = apply(E, 0, (W + 2, 4, (X - 4) // 4, 4), None, (zero, zero))
 
     arrive(lambda dx, dy: dx != 0)
-    extract(0, W, 4)
-    extract(W + X, W, 4)
+    extract(lambda t, p: p + p // W * X, 1)
     sigma(E, (0, X + W, 2, 4), row_groups(0, PY))
     for field in (0, 1):
         for up in (0, 1):
@@ -359,9 +391,9 @@
             def _():
                 phase2(up, field).wait_recv()
     sigma(K, (0, 4, LAYERS // 2, 4), row_groups(0, PX))
-    s0 = diagonal(K, (1, LAYERS, 2, 10), (3, 4, 5, 6), zero)
-    s12 = apply(K, 0, (2, LAYERS, 2, 8), (2, 3, 4, 5), (zero, zero))
-    s34 = apply(K, 1, (3, LAYERS, 2, 6), (1, 2, 3, 4), (zero, zero))
+    s0 = diagonal(K, (lambda t: 1 + 2 * t + (t // 5) * 2, 0, 10, 2), "ask", zero)
+    s12 = apply(K, 0, (lambda t: 2 + 4 * t + (t // 2) * 4, 0, 4, 4), "ask", (zero, zero))
+    s34 = apply(K, 1, (lambda t: 3 + 3 * t + (t // 2) * 6, 0, 4, 3), "ask", (zero, zero))
     s5, _ = apply(K, 2, (4, LAYERS, 2, 4), None, (zero, zero))
     k_sums = [s0, *s12, *s34, s5]
 
@@ -371,8 +403,8 @@
     def complete():
         for k in range(3):
             for j in range(4):
-                kint[pl.ds(j, X, stride=8), :] = K.v[k][pl.ds((LAYERS + 4 + j) * PX + W, X), :]
-                kint[pl.ds(4 + j, X, stride=8), :] = K.v[k][pl.ds((4 + j) * PX + W, X), :]
+                kint[pl.ds(j, X, stride=8), :] = k_arr[K.v[k].rows(LAYERS + 4 + j, W, X)]
+                kint[pl.ds(4 + j, X, stride=8), :] = k_arr[K.v[k].rows(4 + j, W, X)]
             for q in range(blocks):
                 kt[k, q] = kint[128 * q:128 * q + 128, :].T
 
@@ -380,7 +412,7 @@
             for k in range(3):
                 for s in range(W, W + Y, 8):
                     turned = pltpu.roll(kt[k, m // 16, pl.ds(s, 8), :], lax.rem(252 - 8 * lax.rem(m, 16), 128), 1)
-                    E.v[k][m + W, pl.ds(s, 8), :] = jnp.where(edge, turned, E.v[k][m + W, pl.ds(s, 8), :])
+                    E.v[k][m + W, s] = jnp.where(edge, turned, E.v[k][m + W, s])
             return c
         lax.fori_loop(0, X, body, 0, unroll=2)
 
@@ -425,13 +457,26 @@
     c1 = safe(y1, d1) - l21 * c2
     c0 = safe(n[0], a[0]) - l1 * c1 - l2 * c2
 
-    def finish(m, c):
-        for s in range(0, Y, 8):
-            out[m, pl.ds(s, 8), :] = (c0 * E.v[0][m + W, pl.ds(s + W, 8), :] + c1 * E.v[1][m + W, pl.ds(s + W, 8), :]
-                                      + c2 * E.v[2][m + W, pl.ds(s + W, 8), :])
+    quarter = X // 4
+
+    def put(t):
+        part = pl.ds(t * quarter, quarter)
+        return pltpu.make_async_copy(out.at[part], out_any.at[part], out_sem.at[t])
+
+    def finish(t, c):
+        for u in range(2):
+            m = 2 * t + u
+            for s in range(0, Y, 8):
+                out[m, pl.ds(s, 8), :] = (c0 * E.v[0][m + W, s + W] + c1 * E.v[1][m + W, s + W]
+                                          + c2 * E.v[2][m + W, s + W])
         return c
 
-    lax.fori_loop(0, X, finish, 0, unroll=2)
+    def chunk(t, c):
+        lax.fori_loop(t * (quarter // 2), (t + 1) * (quarter // 2), finish, 0)
+        put(t).start()
+        return c
+
+    lax.fori_loop(0, 4, chunk, 0)
 
     for field in (0, 1):
         for i, (dx, dy) in enumerate(DIRS):
@@ -443,13 +488,16 @@
             def _():
                 phase2(up, field).wait_send()
 
+    for t in range(4):
+        put(t).wait()
+
 
 def local(labels, conductivity, right_side, sizes):
     gxn, gyn, gzn = sizes
     X, Y, Z = labels.shape
     assert Z == 128 and Y % 8 == 0
     PX, PY = X + 2 * W, Y + 2 * W
-    krows = 2 * LAYERS * PX
+    krows = 2 * LAYERS * (PX + 1)
     f32 = jnp.float32
     count = {"gx": gxn, "gy": gyn, "gz": gzn}
     slots = sum(math.prod(count[a] for a in axes) - 1 for axes in STAGES)
@@ -458,24 +506,25 @@
         functools.partial(kernel, (gxn, gyn, gzn, X, Y)),
         out_shape=jax.ShapeDtypeStruct((X, Y, Z), f32),
         in_specs=[
-            pl.BlockSpec(memory_space=pltpu.SMEM),
-            pl.BlockSpec(memory_space=pl.ANY),
-            pl.BlockSpec(memory_space=pl.ANY),
+            pl.BlockSpec(memory_space=pltpu.HBM),
+            pl.BlockSpec(memory_space=pltpu.HBM),
+            pl.BlockSpec(memory_space=pltpu.HBM),
         ],
-        out_specs=pl.BlockSpec(memory_space=pltpu.VMEM),
+        out_specs=pl.BlockSpec(memory_space=pl.ANY),
         scratch_shapes=[
             pltpu.VMEM((PX, PY, 128), jnp.int32),
             pltpu.VMEM((PX, PY, 128), f32),
-            pltpu.VMEM((21, PX, PY, 128), f32),
+            pltpu.VMEM((18 * (PX * PY + SKEW), 128), f32),
             pltpu.VMEM((krows, 128), jnp.int32),
             pltpu.VMEM((krows, 128), f32),
-            pltpu.VMEM((21, krows, 128), f32),
+            pltpu.VMEM((18 * (krows + SKEW), 128), f32),
             pltpu.VMEM((-(-X // 16) * 128, 128), f32),
             pltpu.VMEM((3, -(-X // 16), 128, 128), f32),
             pltpu.VMEM((3, 8, 128), f32),
             pltpu.VMEM((slots, 128), f32),
-            dma((2,)), dma((8, 2)), dma((8, 2)), dma((2, 2)), dma((2, 2)), dma((slots,)), dma((slots,)),
-            pltpu.SemaphoreType.REGULAR((2,)),
+            dma((3,)), dma((8, 2)), dma((8, 2)), dma((2, 2)), dma((2, 2)), dma((slots,)), dma((slots,)),
+            pltpu.SemaphoreType.REGULAR((2,)), pltpu.VMEM((X, Y, Z), f32), dma((4,)),
+            pltpu.SMEM((7, 8), f32),
         ],
         compiler_params=pltpu.CompilerParams(
             collective_id=0, has_side_effects=True, vmem_limit_bytes=62 * 1024 * 1024),

time: 41.3 us -> 39.1 us (0.947)
  Pallas kernels: 38.8 us -> 36.6 us
    pallas_call x1, Pallas kernels: 38.8 us -> 36.6 us  [local(): pl.pallas_call(functools.partial(kernel, (gxn, gyn, gzn, X, Y)), out_shap...]
where the time goes in v3:
time: 39.1 us; the launch traced here: 38.9 us
  Pallas kernels  36.6 us (94%)
  local copies, waits for them, and re-layouts  2.31 us (6%)
    pallas_call x1, Pallas kernels, local(): pl.pallas_call(functools.partial(kernel, (gxn, gyn, gzn, X, Y)), out_shap...  36.6 us
    unnamed x1, local copies, waits for them, and re-layouts  2.31 us

profile of v3, /device:TPU:0, one launch (start us, length us, event | category | flops | bytes accessed | tf_op | source)
XLA Modules:
  0.0 38.9 jit_solution(11172029479099691824)
XLA Ops:
  0.0 36.6 %shard_map.37 = f32[32,64,128]{2,1,0:T(8,128)} custom-call(f32[7,8]{1,0:T(8,128)} %cond_hbm.1, s32[32,64,128]{2,1,0:T(8,128)} %lab_hbm.1, f32[32,64,128]{2,1,0:T(8,128)} %b_hbm.1), custom_call_target="tpu_custom_call" | custom-call | tf_op jit(solution)/shard_map/pallas_call | solution.py:505
  36.6 2.3 %copy.5 = f32[32,64,128]{2,1,0:T(8,128)} copy(f32[32,64,128]{2,1,0:T(8,128)} %shard_map.37) | data formatting | bytes 2097152

commit v4 on v3

--- a/solution.py
+++ b/solution.py
@@ -15,7 +15,7 @@
 SKEW = 8
 OUTSIDE = 8
 DIRS = ((0, -1), (0, 1), (-1, 0), (1, 0), (-1, -1), (-1, 1), (1, -1), (1, 1))
-STAGES = (("gx", "gy"), ("gz",))
+STAGES = (("gy",), ("gx", "gz"))
 
 
 def row_groups(lo, hi):
@@ -60,7 +60,8 @@
     ring = {"gx": (gx, gxn), "gy": (gy, gyn), "gz": (gz, gzn)}
 
     def peers_of(axes):
-        return [d for d in itertools.product(*[range(ring[a][1]) for a in axes]) if any(d)]
+        far = lambda d: sum(min(k, ring[a][1] - k) for a, k in zip(axes, d))
+        return sorted((d for d in itertools.product(*[range(ring[a][1]) for a in axes]) if any(d)), key=far, reverse=True)
 
     def peer(axes, d):
         return {a: lax.rem(ring[a][0] + k, ring[a][1]) for a, k in zip(axes, d) if k}
@@ -425,6 +426,7 @@
 
     pl.semaphore_wait(greet.at[0], gxn - 1)
     slot = 0
+    sent = []
     for stage, axes in enumerate(STAGES):
         ar[stage] = jnp.broadcast_to(row, (8, 128))
         copies = []
@@ -441,8 +443,7 @@
         for copy in copies:
             copy.wait_recv()
         row = row + jnp.sum(arslot[first:slot, :], axis=0, keepdims=True)
-        for copy in copies:
-            copy.wait_send()
+        sent += copies
 
     n = [jnp.broadcast_to(row[:, k:k + 1], (8, 128)) for k in range(6)]
     a = [n[k] - n[k + 1] for k in range(5)]
@@ -478,6 +479,8 @@
 
     lax.fori_loop(0, 4, chunk, 0)
 
+    for copy in sent:
+        copy.wait_send()
     for field in (0, 1):
         for i, (dx, dy) in enumerate(DIRS):
             @pl.when(exists(dx, dy))

time: 39.1 us -> 38.7 us (0.990)
  no operation moved by 1% of the time
where the time goes in v4:
time: 38.7 us; the launch traced here: 38.6 us
  Pallas kernels  36.3 us (94%)
  local copies, waits for them, and re-layouts  2.31 us (6%)
    pallas_call x1, Pallas kernels, local(): pl.pallas_call(functools.partial(kernel, (gxn, gyn, gzn, X, Y)), out_shap...  36.3 us
    unnamed x1, local copies, waits for them, and re-layouts  2.31 us

profile of v4, /device:TPU:0, one launch (start us, length us, event | category | flops | bytes accessed | tf_op | source)
XLA Modules:
  0.0 38.6 jit_solution(3808216954780477076)
XLA Ops:
  0.0 36.3 %shard_map.37 = f32[32,64,128]{2,1,0:T(8,128)} custom-call(f32[7,8]{1,0:T(8,128)} %cond_hbm.1, s32[32,64,128]{2,1,0:T(8,128)} %lab_hbm.1, f32[32,64,128]{2,1,0:T(8,128)} %b_hbm.1), custom_call_target="tpu_custom_call" | custom-call | tf_op jit(solution)/shard_map/pallas_call | solution.py:508
  36.3 2.3 %copy.5 = f32[32,64,128]{2,1,0:T(8,128)} copy(f32[32,64,128]{2,1,0:T(8,128)} %shard_map.37) | data formatting | bytes 2097152
